TPU v7x, 768 devices: a whole 4x8x12 slice. The times are simulated.
768 devices in a mesh: seq: 64 (over y, x, core), head: 12 (over z).
Axes of the slice: x: 4, y: 8, z: 12, core: 2. Of those that a mesh axis runs over, the one named last changes fastest.
Arguments:
- query_raw: float32 [16384, 48, 128], P('seq', 'head'), may hold values from -150 to 150
- key_raw: float32 [16384, 48, 128], P('seq', 'head'), may hold values from -150 to 150
- value_raw: float32 [16384, 48, 128], P('seq', 'head'), may hold values from -6 to 6
- query_gain: float32 [48, 128], P('head'), may hold values from 0.25 to 1.75
- key_gain: float32 [48, 128], P('head'), may hold values from 0.25 to 1.75
- cotangent: float32 [16384, 48, 128], P('seq', 'head'), may hold values from -6 to 6
Outputs:
- attended: float32 [16384, 48, 128], P('seq', 'head')
- grad_query: float32 [16384, 48, 128], P('seq', 'head')
- grad_key: float32 [16384, 48, 128], P('seq', 'head')
- grad_value: float32 [16384, 48, 128], P('seq', 'head')
All inputs are finite; a program needn't handle non-finite values.
Results may differ from a plain program's by a relative error of at most 0.00023.
Values sent between devices are 32-bit elements; how exact they have to be, the bound alone decides.
A program may use at most 64 MiB of HBM per device.

v0:
```python
import jax
import jax.numpy as jnp
from jax import lax
from jax.sharding import Mesh
from jax.sharding import PartitionSpec as P

SEQ = ("seq_0", "seq_1", "seq_2")


epsilon = 1e-06
highest = lax.Precision.HIGHEST


def sent_to_all(x, axis):
    count = lax.axis_size(axis)
    return lax.all_to_all(jnp.broadcast_to(x[None], (count, *x.shape)), axis, 0, 0, tiled=True)


def of_everyone(x, axis):
    return sent_to_all(x, axis).sum(axis=0)


def in_one(arrays, axis):
    line, at, finished = (jnp.concatenate([a.reshape(-1) for a in arrays]), 0, [])
    total = of_everyone(line, axis)
    for a in arrays:
        finished.append(total[at : at + a.size].reshape(a.shape))
        at += a.size
    return tuple(finished)


def neutral_like(x, identity):
    return jnp.broadcast_to(jnp.asarray(identity, x.dtype), x.shape)


def entering(x, axes, combine, identity, reverse):
    before = start = neutral_like(x, identity)
    total = x
    for axis in reversed(axes):
        count, here = (lax.axis_size(axis), lax.axis_index(axis))
        pieces = lax.all_gather(total, axis)
        inside, total = (start, start)
        for k in reversed(range(count)) if reverse else range(count):
            passed = k > here if reverse else k < here
            total = combine(total, pieces[k])
            inside = jnp.where(passed, total, inside)
        before = combine(inside, before)
    return before


def product(form, left, right):
    return jnp.einsum(form, left, right, precision=highest, preferred_element_type=jnp.float32)


def add_states(earlier, later):
    return earlier + later


def local(query_raw, key_raw, value_raw, query_gain, key_gain, cotangent):
    tok_rows = query_raw.shape[0]
    head_size = query_raw.shape[2]
    full_width = query_raw.shape[1] * head_size * lax.axis_size("head")
    query_squares = jnp.sum(query_raw * query_raw, axis=(1, 2))
    key_squares = jnp.sum(key_raw * key_raw, axis=(1, 2))
    query_total, key_total = in_one((query_squares, key_squares), "head")
    query_scale = lax.rsqrt(query_total / full_width + epsilon)
    key_scale = lax.rsqrt(key_total / full_width + epsilon)
    query_unit = query_raw * query_scale[:, None, None]
    key_unit = key_raw * key_scale[:, None, None]
    query_hat = query_unit * query_gain[None]
    key_hat = key_unit * key_gain[None]
    tok_index = jnp.arange(tok_rows)
    position = (lax.axis_index(SEQ) * tok_rows + tok_index).astype(jnp.float32)
    position_weight = lax.rsqrt(float(head_size) * (position + 1.0))
    grad_scaled = cotangent * position_weight[:, None, None]
    local_state = product("thd,the->hde", key_hat, value_raw)
    local_grad = product("thd,the->hde", query_hat, grad_scaled)
    zero_state = jnp.zeros_like(local_state)
    earlier = entering(local_state, SEQ, add_states, zero_state, False)
    later = entering(local_grad, SEQ, add_states, zero_state, True)
    causal = tok_index[:, None] >= tok_index[None, :]
    scores = jnp.where(causal[None], product("thd,shd->hts", query_hat, key_hat), 0.0)
    attended = product("hts,she->the", scores, value_raw) + product(
        "thd,hde->the", query_hat, earlier
    )
    attended = attended * position_weight[:, None, None]
    mixing = jnp.where(causal[None], product("the,she->hts", grad_scaled, value_raw), 0.0)
    grad_qhat = product("hts,shd->thd", mixing, key_hat) + product(
        "the,hde->thd", grad_scaled, earlier
    )
    grad_khat = product("hts,thd->shd", mixing, query_hat) + product(
        "she,hde->shd", value_raw, later
    )
    grad_value = product("hts,the->she", scores, grad_scaled) + product(
        "shd,hde->she", key_hat, later
    )
    query_push = grad_qhat * query_gain[None]
    key_push = grad_khat * key_gain[None]
    query_along = jnp.sum(query_unit * query_push, axis=(1, 2))
    key_along = jnp.sum(key_unit * key_push, axis=(1, 2))
    query_inner, key_inner = in_one((query_along, key_along), "head")
    grad_query = query_scale[:, None, None] * (
        query_push - query_unit * (query_inner / full_width)[:, None, None]
    )
    grad_key = key_scale[:, None, None] * (
        key_push - key_unit * (key_inner / full_width)[:, None, None]
    )
    return (attended, grad_query, grad_key, grad_value)


def solution(mesh):
    finer = Mesh(
        mesh.devices.reshape(8, 4, 2, mesh.shape["head"]), ("seq_0", "seq_1", "seq_2", "head")
    )
    return jax.shard_map(
        local,
        mesh=finer,
        in_specs=(
            P(SEQ, "head", None),
            P(SEQ, "head", None),
            P(SEQ, "head", None),
            P("head", None),
            P("head", None),
            P(SEQ, "head", None),
        ),
        out_specs=(
            P(SEQ, "head", None),
            P(SEQ, "head", None),
            P(SEQ, "head", None),
            P(SEQ, "head", None),
        ),
        check_vma=False,
    )
```

profile of v0, /device:TPU:6, one launch (start us, length us, event | category | flops | bytes accessed | tf_op | source)
XLA Modules:
  0.0 236.8 jit_solution(14272193196122814956)
XLA Ops:
  7.2 2.3 multiply_reduce_fusion.2
  9.5 0.6 broadcast_in_dim.25
  10.1 15.2 %all-to-all-start = ((f32[12,1,512]{2,1,0:T(1,128)}), f32[12,1,512]{2,1,0:T(1,128)S(1)}, u32[]{:S(2)}, u32[]{:S(2)}) async-start(f32[12,1,512]{2,1,0:T(1,128)} %broadcast_in_dim.25), calls=%async_computation | async-start | bytes 49152 | tf_op jit(solution)/shard_map/all_to_all | solution.py:16
  25.3 0.0 all-gather.13.cloned.1.call-start
  25.3 1.3 copy.49
  26.6 9.1 %all-to-all-done = f32[12,1,512]{2,1,0:T(1,128)S(1)} async-done(((f32[12,1,512]{2,1,0:T(1,128)}), f32[12,1,512]{2,1,0:T(1,128)S(1)}, u32[]{:S(2)}, u32[]{:S(2)}) %all-to-all-start) | async-done | bytes 24608 | tf_op jit(solution)/shard_map/all_to_all | solution.py:16
  35.8 0.7 fusion.10
  36.6 2.2 all-gather
  38.7 0.8 slice_add_fusion.21
  39.5 0.0 all-gather.13.cloned.1.call-update
  39.6 0.0 all-gather.15.cloned.1.call-start
  39.6 0.2 copy.48
  39.9 0.8 fusion.13
  40.7 2.2 all-gather.1
  42.9 0.8 copy-done.4
  43.7 0.7 slice_add_fusion.10
  44.4 0.0 all-gather.15.cloned.1.call-update
  44.4 0.0 all-gather.9.cloned.1.call-start
  44.5 20.5 %all-gather.13.cloned.1.call-done = f32[16,128,128]{2,1,0:T(8,128)} async-done(((f32[4,128,128]{2,1,0:T(8,128)}), f32[16,128,128]{2,1,0:T(8,128)}) %all-gather.13.cloned.1.call-update) | async-done | bytes 1048592 | tf_op jit(solution)/shard_map/all_gather | solution.py:41
  64.9 1.9 fusion.23
  66.9 0.0 all-gather.9.cloned.1.call-update
  66.9 0.2 all-gather.11.cloned.1.call-start
  67.1 33.4 %all-gather.15.cloned.1.call-done = f32[16,128,128]{2,1,0:T(8,128)} async-done(((f32[4,128,128]{2,1,0:T(8,128)}), f32[16,128,128]{2,1,0:T(8,128)}) %all-gather.15.cloned.1.call-update) | async-done | bytes 1048592 | tf_op jit(solution)/shard_map/all_gather | solution.py:41
  100.5 1.9 fusion.19
  102.5 0.0 all-gather.11.cloned.1.call-update
  102.6 2.1 convolution_select_fusion
  104.7 1.3 convolution_select_fusion.1
  105.9 45.0 %all-gather.9.cloned.1.call-done = f32[8,4,128,128]{3,2,1,0:T(8,128)} async-done(((f32[1,4,128,128]{3,2,1,0:T(8,128)}), f32[8,4,128,128]{3,2,1,0:T(8,128)}) %all-gather.9.cloned.1.call-update) | async-done | bytes 2097168 | tf_op jit(solution)/shard_map/all_gather | solution.py:41
  150.9 2.3 fusion.22
  153.3 1.5 fusion.15
  154.7 1.9 convolution_bitcast_fusion
  156.7 42.0 %all-gather.11.cloned.1.call-done = f32[8,4,128,128]{3,2,1,0:T(8,128)} async-done(((f32[1,4,128,128]{3,2,1,0:T(8,128)}), f32[8,4,128,128]{3,2,1,0:T(8,128)}) %all-gather.11.cloned.1.call-update) | async-done | bytes 2097168 | tf_op jit(solution)/shard_map/all_gather | solution.py:41
  198.7 2.3 fusion.18
  201.0 1.6 fusion.14
  202.5 0.6 fusion.7
  203.2 1.6 multiply_reduce_fusion
  204.8 2.0 multiply_reduce_fusion.1
  206.8 0.6 broadcast_in_dim.28
  207.4 10.2 %all-to-all-start.1 = ((f32[12,1,512]{2,1,0:T(1,128)}), f32[12,1,512]{2,1,0:T(1,128)S(1)}, u32[]{:S(2)}, u32[]{:S(2)}) async-start(f32[12,1,512]{2,1,0:T(1,128)} %broadcast_in_dim.28), calls=%async_computation.1 | async-start | bytes 49152 | tf_op jit(solution)/shard_map/all_to_all | solution.py:16
  217.6 3.0 %fusion = f32[256,4,128]{0,2,1:T(8,128)} fusion(f32[4,128,256]{2,1,0:T(8,128)} %fusion.14, f32[4,256,256]{2,1,0:T(8,128)S(1)} %convolution_select_fusion.1, f32[256,4,128]{2,1,0:T(4,128)S(1)} %copy-done.2, f32[256]{0:T(256)S(1)} %multiply_rsqrt_fusion), kind=kOutput, calls=%fused_computation.3 | convolution fusion | flops 402915328 | bytes 2622464 | tf_op jit(solution)/shard_map/hts,the->she/dot_general | solution.py:52
  220.7 1.1 fusion.6
  221.8 1.1 copy.63
  222.9 2.1 copy.66
  225.0 3.1 %all-to-all-done.1 = f32[12,1,512]{2,1,0:T(1,128)S(1)} async-done(((f32[12,1,512]{2,1,0:T(1,128)}), f32[12,1,512]{2,1,0:T(1,128)S(1)}, u32[]{:S(2)}, u32[]{:S(2)}) %all-to-all-start.1) | async-done | bytes 24608 | tf_op jit(solution)/shard_map/all_to_all | solution.py:16
  228.1 0.1 subtract_multiply_fusion
  228.2 1.0 copy.65
  229.2 0.1 subtract_multiply_fusion.1
  229.3 1.0 copy.64
  (31 shorter events, 0.2 us)
Async XLA Ops:
  7.2 28.6 %copy-start = (f32[256,4,128]{2,1,0:T(4,128)S(1)}, f32[256,4,128]{2,1,0:T(4,128)}, u32[]{:S(2)}) copy-start(f32[256,4,128]{2,1,0:T(4,128)} %param.8) | copy-start | bytes 1572868
  7.2 28.6 %copy-start.10 = (f32[4,128]{1,0:T(4,128)S(1)}, f32[4,128]{1,0:T(4,128)}, u32[]{:S(2)}) copy-start(f32[4,128]{1,0:T(4,128)} %param.10) | copy-start | bytes 6148
  10.1 25.6 %all-to-all-start = ((f32[12,1,512]{2,1,0:T(1,128)}), f32[12,1,512]{2,1,0:T(1,128)S(1)}, u32[]{:S(2)}, u32[]{:S(2)}) async-start(f32[12,1,512]{2,1,0:T(1,128)} %broadcast_in_dim.25), calls=%async_computation | async-start | bytes 49152 | tf_op jit(solution)/shard_map/all_to_all | solution.py:16
  25.3 14.3 %copy-start.9 = (f32[256,4,128]{2,1,0:T(4,128)S(1)}, f32[256,4,128]{2,1,0:T(4,128)}, u32[]{:S(2)}) copy-start(f32[256,4,128]{2,1,0:T(4,128)} %param.6) | copy-start | bytes 1572868
  25.3 39.6 %all-gather.13.cloned.1.call-start = ((), (), s32[]{:S(2)}) async-start(), calls=%async_computation.4 | async-start | bytes 1310720 | tf_op jit(solution)/shard_map/all_gather | solution.py:41
  35.8 4.1 %copy-start.2 = (f32[256,4,128]{2,1,0:T(4,128)S(1)}, f32[256,4,128]{2,1,0:T(4,128)}, u32[]{:S(2)}) copy-start(f32[256,4,128]{2,1,0:T(4,128)} %param.11) | copy-start | bytes 1572868
  35.8 4.1 %copy-start.11 = (f32[4,128]{1,0:T(4,128)S(1)}, f32[4,128]{1,0:T(4,128)}, u32[]{:S(2)}) copy-start(f32[4,128]{1,0:T(4,128)} %param.9) | copy-start | bytes 6148
  38.7 0.9 copy-start.3
  39.6 61.0 %all-gather.15.cloned.1.call-start = ((), (), s32[]{:S(2)}) async-start(), calls=%async_computation.5 | async-start | bytes 1310720 | tf_op jit(solution)/shard_map/all_gather | solution.py:41
  42.9 0.8 copy-start.4
  44.4 106.5 %all-gather.9.cloned.1.call-start = ((), (), s32[]{:S(2)}) async-start(), calls=%async_computation.2 | async-start | bytes 2359296 | tf_op jit(solution)/shard_map/all_gather | solution.py:41
  66.9 131.7 %all-gather.11.cloned.1.call-start = ((), (), s32[]{:S(2)}) async-start(), calls=%async_computation.3 | async-start | bytes 2359296 | tf_op jit(solution)/shard_map/all_gather | solution.py:41
  201.0 2.2 copy-start.1
  202.5 2.3 copy-start.8
  207.4 20.6 %all-to-all-start.1 = ((f32[12,1,512]{2,1,0:T(1,128)}), f32[12,1,512]{2,1,0:T(1,128)S(1)}, u32[]{:S(2)}, u32[]{:S(2)}) async-start(f32[12,1,512]{2,1,0:T(1,128)} %broadcast_in_dim.28), calls=%async_computation.1 | async-start | bytes 49152 | tf_op jit(solution)/shard_map/all_to_all | solution.py:16
  217.6 3.0 %copy-start.5 = (f32[256,4,128]{2,0,1:T(8,128)S(1)}, f32[256,4,128]{2,0,1:T(8,128)}, u32[]{:S(2)}) copy-start(f32[256,4,128]{2,0,1:T(8,128)} %convolution_bitcast_fusion) | copy-start | bytes 1572868
  221.7 6.4 %copy-start.7 = (f32[256,4,128]{0,2,1:T(8,128)S(1)}, f32[256,4,128]{0,2,1:T(8,128)}, u32[]{:S(2)}) copy-start(f32[256,4,128]{0,2,1:T(8,128)} %get-tuple-element.21) | copy-start | bytes 1572868
  222.9 6.3 %copy-start.6 = (f32[256,4,128]{0,2,1:T(8,128)S(1)}, f32[256,4,128]{0,2,1:T(8,128)}, u32[]{:S(2)}) copy-start(f32[256,4,128]{0,2,1:T(8,128)} %get-tuple-element.23) | copy-start | bytes 1572868
Sparse Core Ops, SparseCore 0:
  39.7 25.2 all-gather.12
  67.9 32.5 all-gather.14
  103.5 47.4 all-gather.8
  153.7 44.8 all-gather.10
where the time goes:
time: 237 us
  waiting for transfers between devices  153 us (65%)
  starting transfers between devices  25.7 us (11%)
  matrix products  18.1 us (8%)
  between operations  14.1 us (6%)
  other arithmetic  12.6 us (5%)
  local copies, waits for them, and re-layouts  8.81 us (4%)
  blocking collectives  4.36 us (2%)
    all_gather x4, waiting for transfers between devices, entering(): pieces = lax.all_gather(total, axis)  141 us
    all_to_all x2, starting transfers between devices, sent_to_all(): lax.all_to_all(jnp.broadcast_to(x[None], (count, *x.shape)), axis, 0, 0,...  25.3 us
    dot_general x12, matrix products, product(): jnp.einsum(form, left, right, precision=highest, preferred_element_type=j...  18.1 us
    all_to_all x2, waiting for transfers between devices, sent_to_all(): lax.all_to_all(jnp.broadcast_to(x[None], (count, *x.shape)), axis, 0, 0,...  12.2 us
    add x6, other arithmetic, add_states(): return earlier + later  10 us
    unnamed x30, local copies, waits for them, and re-layouts  7.58 us
  transfers between devices with their start and end apart: 6, of which 6 were waited for; matrix products, arithmetic and copies ran while one was open for 10% of the time, Pallas kernels for 0%

commit v1 on v0

v1 whole, which is shorter than its diff:
```python
import functools

import jax
import jax.numpy as jnp
from jax import lax
from jax.experimental import pallas as pl
from jax.experimental.pallas import tpu as pltpu
from jax.sharding import PartitionSpec as P

MESH = pl.DeviceIdType.MESH
EPSILON = 1e-06
F32, BF16 = jnp.float32, jnp.bfloat16

NN = ((1,), (0,))
NT = ((1,), (1,))
TN = ((0,), (0,))


def halves(x):
    high = x.astype(BF16)
    return high, (x - high.astype(F32)).astype(BF16)


def product(left, right, form):
    left_high, left_low = halves(left)
    right_high, right_low = halves(right)
    left_parts = jnp.concatenate([left_high, left_low, left_high], axis=form[0][0])
    right_parts = jnp.concatenate([right_high, right_high, right_low], axis=form[1][0])
    return lax.dot_general(left_parts, right_parts, (form, ((), ())), preferred_element_type=F32)


def lane_sums(x):
    high, low = halves(x)
    rest = (x - high.astype(F32) - low.astype(F32)).astype(BF16)
    parts = jnp.concatenate([high, low, rest], axis=1)
    ones = jnp.ones((8, parts.shape[1]), BF16)
    return lax.dot_general(ones, parts, (NT, ((), ())), preferred_element_type=F32)


def kernel(
    n_seq, n_head, heads, tokens, depth,
    q_hbm, k_hbm, v_hbm, c_hbm, q_gain, k_gain,
    att_ref, gq_ref, gk_ref, gv_ref,
    raw, unit, other, first, second, mix, score, weight, scales,
    z_send, z_recv, states, peer, chip_sum, gathered, prefixes, entering, passed, received,
    load_sem, z_sems, core_sems, scan_sems,
):
    chips = n_seq // 2
    share = heads * depth // chips
    seq, head = lax.axis_index("seq"), lax.axis_index("head")
    chip, core = seq // 2, seq % 2
    width = float(heads * n_head * depth)

    loads = [
        pltpu.make_async_copy(src, raw.at[i], load_sem.at[i])
        for i, src in enumerate((q_hbm, k_hbm, v_hbm, c_hbm))
    ]
    for load in loads:
        load.start()

    barrier = pltpu.get_barrier_semaphore()

    def greet_head(d, _):
        pl.semaphore_signal(
            barrier, inc=1, device_id=(seq, lax.rem(head + d, n_head)), device_id_type=MESH
        )
        return 0

    def greet_chip(d, _):
        to = lax.rem(chip + d, chips)
        pl.semaphore_signal(barrier, inc=1, device_id=(2 * to + core, head), device_id_type=MESH)
        return 0

    lax.fori_loop(1, n_head, greet_head, 0)
    lax.fori_loop(1, chips, greet_chip, 0)
    partner = (2 * chip + 1 - core, head)
    pl.semaphore_signal(barrier, inc=1, device_id=partner, device_id_type=MESH)

    def rows_of(h):
        return pl.ds(h, tokens, stride=heads)

    def share_sums(slot, of_query, of_key):
        send, recv = z_send.at[slot], z_recv.at[slot]
        for i, of_one in enumerate((of_query, of_key)):
            sums = lane_sums(of_one)
            for j in range(tokens // 128):
                send[pl.ds(2 * i + j, 1), :] = sums[0:1, 128 * j : 128 * (j + 1)]
        recv[head] = send[...]

    def share_copy(slot, d):
        return pltpu.make_async_remote_copy(
            src_ref=z_send.at[slot],
            dst_ref=z_recv.at[slot, head],
            send_sem=z_sems.at[2 * slot],
            recv_sem=z_sems.at[2 * slot + 1],
            device_id=(seq, lax.rem(head + d, n_head)),
            device_id_type=MESH,
        )

    def send_shares(slot):
        def body(i, _):
            step = (i + 1) // 2
            share_copy(slot, n_head // 2 + step * (1 - 2 * (i % 2))).start()
            return 0

        lax.fori_loop(0, n_head - 1, body, 0)

    def await_shares(slot):
        all_of = z_recv.at[slot, pl.ds(0, n_head - 1)]
        pltpu.make_async_copy(all_of, all_of, z_sems.at[2 * slot]).wait()
        pltpu.make_async_copy(all_of, all_of, z_sems.at[2 * slot + 1]).wait()
        return jnp.sum(z_recv[slot], axis=0)

    def down_rows(line, i):
        return jnp.concatenate(
            [
                jnp.broadcast_to(line[2 * i + j : 2 * i + j + 1, :], (128, 128)).T
                for j in range(tokens // 128)
            ],
            axis=0,
        )

    loads[0].wait()
    loads[1].wait()
    query_squares = jnp.zeros((tokens, depth), F32)
    key_squares = jnp.zeros((tokens, depth), F32)
    for h in range(heads):
        q, k = raw[0, rows_of(h), :], raw[1, rows_of(h), :]
        query_squares += q * q
        key_squares += k * k
    share_sums(0, query_squares, key_squares)

    pl.semaphore_wait(barrier, n_head - 1 + chips - 1 + 1)
    send_shares(0)

    loads[2].wait()
    loads[3].wait()
    position = (seq * tokens + lax.broadcasted_iota(jnp.int32, (tokens, depth), 0)).astype(F32)
    weight[...] = lax.rsqrt(float(depth) * (position + 1.0))
    for h in range(heads):
        other[0, h] = raw[3, rows_of(h), :] * weight[...]
        other[1, h] = raw[2, rows_of(h), :]

    rows = lax.broadcasted_iota(jnp.int32, (tokens, tokens), 0)
    columns = lax.broadcasted_iota(jnp.int32, (tokens, tokens), 1)
    causal = rows >= columns

    def mixing(h, _):
        mix[h] = jnp.where(causal, product(other[0, h], other[1, h], NT), 0.0)
        return 0

    lax.fori_loop(0, heads, mixing, 0)

    total = await_shares(0)
    scale = lax.rsqrt(total / width + EPSILON)
    for i in range(2):
        scales[i] = down_rows(scale, i)
    for i, gain in enumerate((q_gain, k_gain)):
        for h in range(heads):
            unit[i, h] = raw[i, rows_of(h), :] * scales[i] * gain[pl.ds(h, 1), :]

    def block_states(which):
        def body(h, _):
            at = pl.ds(pl.multiple_of(h * depth, depth), depth)
            states[which, at, :] = product(unit[1 - which, h], other[1 - which, h], TN)
            return 0

        lax.fori_loop(0, heads, body, 0)

    def to_partner(src, dst, i):
        return pltpu.make_async_remote_copy(
            src_ref=src,
            dst_ref=dst,
            send_sem=core_sems.at[2 * i],
            recv_sem=core_sems.at[2 * i + 1],
            device_id=partner,
            device_id_type=MESH,
        )

    block_states(1 - core)
    swap = to_partner(states.at[1 - core], peer, 0)
    swap.start()
    block_states(core)
    swap.wait()
    chip_sum[...] = states[core] + peer[...]

    def scan_rows(c):
        return pl.ds(pl.multiple_of(c * share, share), share)

    def scan_copy(src, dst, phase, to):
        return pltpu.make_async_remote_copy(
            src_ref=src,
            dst_ref=dst,
            send_sem=scan_sems.at[2 * phase],
            recv_sem=scan_sems.at[2 * phase + 1],
            device_id=(2 * to + core, head),
            device_id_type=MESH,
        )

    def scatter(i, _):
        to = lax.rem(chip + i, chips)
        scan_copy(chip_sum.at[scan_rows(to)], gathered.at[chip], 0, to).start()
        return 0

    def await_scan(phase):
        all_of = gathered.at[pl.ds(0, chips - 1)]
        pltpu.make_async_copy(all_of, all_of, scan_sems.at[2 * phase]).wait()
        pltpu.make_async_copy(all_of, all_of, scan_sems.at[2 * phase + 1]).wait()

    lax.fori_loop(1, chips, scatter, 0)
    gathered[chip] = chip_sum[scan_rows(chip), :]

    def scoring(h, _):
        score[h] = jnp.where(causal, product(unit[0, h], unit[1, h], NT), 0.0)
        return 0

    lax.fori_loop(0, heads, scoring, 0)
    await_scan(0)

    def prefix(i, running):
        c = i + core * (chips - 1 - 2 * i)
        prefixes[c] = running
        return running + gathered[c]

    lax.fori_loop(0, chips, prefix, jnp.zeros((share, depth), F32))

    def give_back(i, _):
        to = lax.rem(chip + i, chips)
        scan_copy(prefixes.at[to], entering.at[scan_rows(chip)], 1, to).start()
        return 0

    lax.fori_loop(1, chips, give_back, 0)
    entering[scan_rows(chip), :] = prefixes[chip]

    def inside(h, _):
        first[0, h] = product(score[h], other[1, h], NN)
        second[0, h] = product(mix[h], unit[1, h], NN)
        first[1, h] = product(score[h], other[0, h], TN)
        second[1, h] = product(mix[h], unit[0, h], TN)
        return 0

    lax.fori_loop(0, heads, inside, 0)
    await_scan(1)

    passed[...] = entering[...] + states[core]
    hand = to_partner(passed, received, 1)
    hand.start()

    def apply(which, state):
        def body(h, _):
            held = state[pl.ds(pl.multiple_of(h * depth, depth), depth), :]
            first[which, h] += product(unit[which, h], held, NN)
            second[which, h] += product(other[which, h], held, NT)
            return 0

        lax.fori_loop(0, heads, body, 0)

    apply(core, entering)
    hand.wait()
    apply(1 - core, received)

    query_inner = jnp.zeros((tokens, depth), F32)
    key_inner = jnp.zeros((tokens, depth), F32)
    for h in range(heads):
        query_inner += unit[0, h] * second[0, h]
        key_inner += unit[1, h] * second[1, h]
    share_sums(1, query_inner, key_inner)
    send_shares(1)
    for h in range(heads):
        att_ref[rows_of(h), :] = first[0, h] * weight[...]
        gv_ref[rows_of(h), :] = first[1, h]
    mean = await_shares(1) / width
    for i, (gain, out) in enumerate(((q_gain, gq_ref), (k_gain, gk_ref))):
        along = down_rows(mean, i) * scales[i]
        for h in range(heads):
            push = second[i, h] * gain[pl.ds(h, 1), :]
            out[rows_of(h), :] = scales[i] * (push - raw[i, rows_of(h), :] * along)


def local(n_seq, n_head, query_raw, key_raw, value_raw, query_gain, key_gain, cotangent):
    tokens, heads, depth = query_raw.shape
    chips = n_seq // 2
    flat = (tokens * heads, depth)
    states = (heads * depth, depth)
    per_owner = (chips, heads * depth // chips, depth)
    anywhere = pl.BlockSpec(memory_space=pl.ANY)
    vmem = pl.BlockSpec(memory_space=pltpu.VMEM)
    outs = pl.pallas_call(
        functools.partial(kernel, n_seq, n_head, heads, tokens, depth),
        out_shape=[jax.ShapeDtypeStruct(flat, F32)] * 4,
        in_specs=[anywhere] * 4 + [vmem] * 2,
        out_specs=[vmem] * 4,
        scratch_shapes=[
            pltpu.VMEM((4, *flat), F32),
            pltpu.VMEM((2, heads, tokens, depth), F32),
            pltpu.VMEM((2, heads, tokens, depth), F32),
            pltpu.VMEM((2, heads, tokens, depth), F32),
            pltpu.VMEM((2, heads, tokens, depth), F32),
            pltpu.VMEM((heads, tokens, tokens), F32),
            pltpu.VMEM((heads, tokens, tokens), F32),
            pltpu.VMEM((tokens, depth), F32),
            pltpu.VMEM((2, tokens, depth), F32),
            pltpu.VMEM((2, 2 * tokens // 128, 128), F32),
            pltpu.VMEM((2, n_head, 2 * tokens // 128, 128), F32),
            pltpu.VMEM((2, *states), F32),
            pltpu.VMEM(states, F32),
            pltpu.VMEM(states, F32),
            pltpu.VMEM(per_owner, F32),
            pltpu.VMEM(per_owner, F32),
            pltpu.VMEM(states, F32),
            pltpu.VMEM(states, F32),
            pltpu.VMEM(states, F32),
            pltpu.SemaphoreType.DMA((4,)),
            pltpu.SemaphoreType.DMA((4,)),
            pltpu.SemaphoreType.DMA((4,)),
            pltpu.SemaphoreType.DMA((4,)),
        ],
        compiler_params=pltpu.CompilerParams(
            collective_id=0, has_side_effects=True, vmem_limit_bytes=48 * 1024 * 1024
        ),
    )(
        *(x.reshape(flat) for x in (query_raw, key_raw, value_raw, cotangent)),
        query_gain,
        key_gain,
    )
    return tuple(x.reshape(tokens, heads, depth) for x in outs)


def solution(mesh):
    spec, gain = P("seq", "head", None), P("head", None)
    return jax.shard_map(
        functools.partial(local, mesh.shape["seq"], mesh.shape["head"]),
        mesh=mesh,
        in_specs=(spec, spec, spec, gain, gain, spec),
        out_specs=(spec,) * 4,
        check_vma=False,
    )
```

time: 237 us -> 65.5 us (0.28)
  the two profiles are of different devices: /device:TPU:6 before, /device:TPU:1 now
where the time goes in v1:
time: 65.5 us; the launch traced here: 65.1 us
  Pallas kernels  56.4 us (86%)
  local copies, waits for them, and re-layouts  8.02 us (12%)
  between operations  0.66 us (1%)
    pallas_call x1, Pallas kernels, local(): pl.pallas_call(functools.partial(kernel, n_seq, n_head, heads, tokens, de...  56.4 us
    unnamed x16, local copies, waits for them, and re-layouts  8.02 us

profile of v1, /device:TPU:1, one launch (start us, length us, event | category | flops | bytes accessed | tf_op | source)
XLA Modules:
  0.0 65.1 jit_solution(7522103017050084876)
XLA Ops:
  0.6 0.0 copy-start.5
  0.6 0.0 copy-start.4
  0.7 0.7 %copy-done.5 = f32[4,128]{1,0:T(4,128)S(1)} copy-done((f32[4,128]{1,0:T(4,128)S(1)}, f32[4,128]{1,0:T(4,128)}, u32[]{:S(2)}) %copy-start.5) | copy-done | bytes 2072
  1.3 0.0 copy-done.4
  1.3 0.0 copy-start
  1.3 1.0 %copy-done = f32[256,4,128]{2,1,0:T(4,128)S(1)} copy-done((f32[256,4,128]{2,1,0:T(4,128)S(1)}, f32[256,4,128]{2,1,0:T(4,128)}, u32[]{:S(2)}) %copy-start) | copy-done | bytes 524312
  2.4 0.0 copy-start.1
  2.4 1.0 %copy-done.1 = f32[256,4,128]{2,1,0:T(4,128)S(1)} copy-done((f32[256,4,128]{2,1,0:T(4,128)S(1)}, f32[256,4,128]{2,1,0:T(4,128)}, u32[]{:S(2)}) %copy-start.1) | copy-done | bytes 524312
  3.4 0.0 copy-start.2
  3.4 1.0 %copy-done.2 = f32[256,4,128]{2,1,0:T(4,128)S(1)} copy-done((f32[256,4,128]{2,1,0:T(4,128)S(1)}, f32[256,4,128]{2,1,0:T(4,128)}, u32[]{:S(2)}) %copy-start.2) | copy-done | bytes 524312
  4.5 0.0 copy-start.3
  4.5 1.0 %copy-done.3 = f32[256,4,128]{2,1,0:T(4,128)S(1)} copy-done((f32[256,4,128]{2,1,0:T(4,128)S(1)}, f32[256,4,128]{2,1,0:T(4,128)}, u32[]{:S(2)}) %copy-start.3) | copy-done | bytes 524312
  5.5 56.4 %shard_map.93 = (f32[1024,128]{1,0:T(8,128)S(1)}, f32[1024,128]{1,0:T(8,128)S(1)}, f32[1024,128]{1,0:T(8,128)S(1)}, f32[1024,128]{1,0:T(8,128)S(1)}) custom-call(f32[1024,128]{1,0:T(8,128)S(1)} %bitcast.12, f32[1024,128]{1,0:T(8,128)S(1)} %bitcast.13, f32[1024,128]{1,0:T(8,128)S(1)} %bitcast.14, f32[1024,128]{1,0:T(8,128)S(1)} %bitcast.15, ...), custom_call_target="tpu_custom_call" | custom-call | tf_op jit(solution)/shard_map/pallas_call | solution.py:288
  61.9 0.8 %copy.14 = f32[256,4,128]{2,1,0:T(4,128)} copy(f32[256,4,128]{2,1,0:T(4,128)S(1)} %bitcast.11) | data formatting | bytes 1048576
  62.7 0.8 %copy.15 = f32[256,4,128]{2,1,0:T(4,128)} copy(f32[256,4,128]{2,1,0:T(4,128)S(1)} %bitcast.10) | data formatting | bytes 1048576
  63.5 0.8 %copy.16 = f32[256,4,128]{2,1,0:T(4,128)} copy(f32[256,4,128]{2,1,0:T(4,128)S(1)} %bitcast.9) | data formatting | bytes 1048576
  64.3 0.8 %copy.17 = f32[256,4,128]{2,1,0:T(4,128)} copy(f32[256,4,128]{2,1,0:T(4,128)S(1)} %bitcast.8) | data formatting | bytes 1048576
Async XLA Ops:
  0.6 0.7 %copy-start.5 = (f32[4,128]{1,0:T(4,128)S(1)}, f32[4,128]{1,0:T(4,128)}, u32[]{:S(2)}) copy-start(f32[4,128]{1,0:T(4,128)} %k_gain.1) | copy-start | bytes 6148
  0.6 0.7 %copy-start.4 = (f32[4,128]{1,0:T(4,128)S(1)}, f32[4,128]{1,0:T(4,128)}, u32[]{:S(2)}) copy-start(f32[4,128]{1,0:T(4,128)} %q_gain.1) | copy-start | bytes 6148
  1.3 1.0 %copy-start = (f32[256,4,128]{2,1,0:T(4,128)S(1)}, f32[256,4,128]{2,1,0:T(4,128)}, u32[]{:S(2)}) copy-start(f32[256,4,128]{2,1,0:T(4,128)} %param.6) | copy-start | bytes 1572868
  2.4 1.0 %copy-start.1 = (f32[256,4,128]{2,1,0:T(4,128)S(1)}, f32[256,4,128]{2,1,0:T(4,128)}, u32[]{:S(2)}) copy-start(f32[256,4,128]{2,1,0:T(4,128)} %param.7) | copy-start | bytes 1572868
  3.4 1.0 %copy-start.2 = (f32[256,4,128]{2,1,0:T(4,128)S(1)}, f32[256,4,128]{2,1,0:T(4,128)}, u32[]{:S(2)}) copy-start(f32[256,4,128]{2,1,0:T(4,128)} %param.8) | copy-start | bytes 1572868
  4.5 1.0 %copy-start.3 = (f32[256,4,128]{2,1,0:T(4,128)S(1)}, f32[256,4,128]{2,1,0:T(4,128)}, u32[]{:S(2)}) copy-start(f32[256,4,128]{2,1,0:T(4,128)} %param.11) | copy-start | bytes 1572868

commit v2 on v1

--- a/solution.py
+++ b/solution.py
@@ -9,6 +9,7 @@
 
 MESH = pl.DeviceIdType.MESH
 EPSILON = 1e-06
+CHIPS_X = 4
 F32, BF16 = jnp.float32, jnp.bfloat16
 
 NN = ((1,), (0,))
@@ -39,9 +40,9 @@
 
 def kernel(
     n_seq, n_head, heads, tokens, depth,
-    q_hbm, k_hbm, v_hbm, c_hbm, q_gain, k_gain,
+    q_hbm, k_hbm, v_hbm, c_hbm, q_gain_hbm, k_gain_hbm,
     att_ref, gq_ref, gk_ref, gv_ref,
-    raw, unit, other, first, second, mix, score, weight, scales,
+    raw, gains, unit, other, first, second, mix, score, weight, scales,
     z_send, z_recv, states, peer, chip_sum, gathered, prefixes, entering, passed, received,
     load_sem, z_sems, core_sems, scan_sems,
 ):
@@ -54,6 +55,9 @@
     loads = [
         pltpu.make_async_copy(src, raw.at[i], load_sem.at[i])
         for i, src in enumerate((q_hbm, k_hbm, v_hbm, c_hbm))
+    ] + [
+        pltpu.make_async_copy(src, gains.at[i], load_sem.at[4 + i])
+        for i, src in enumerate((q_gain_hbm, k_gain_hbm))
     ]
     for load in loads:
         load.start()
@@ -135,6 +139,8 @@
 
     loads[2].wait()
     loads[3].wait()
+    loads[4].wait()
+    loads[5].wait()
     position = (seq * tokens + lax.broadcasted_iota(jnp.int32, (tokens, depth), 0)).astype(F32)
     weight[...] = lax.rsqrt(float(depth) * (position + 1.0))
     for h in range(heads):
@@ -155,9 +161,9 @@
     scale = lax.rsqrt(total / width + EPSILON)
     for i in range(2):
         scales[i] = down_rows(scale, i)
-    for i, gain in enumerate((q_gain, k_gain)):
+    for i in range(2):
         for h in range(heads):
-            unit[i, h] = raw[i, rows_of(h), :] * scales[i] * gain[pl.ds(h, 1), :]
+            unit[i, h] = raw[i, rows_of(h), :] * scales[i] * gains[i, pl.ds(h, 1), :]
 
     def block_states(which):
         def body(h, _):
@@ -197,17 +203,24 @@
             device_id_type=MESH,
         )
 
-    def scatter(i, _):
-        to = lax.rem(chip + i, chips)
-        scan_copy(chip_sum.at[scan_rows(to)], gathered.at[chip], 0, to).start()
-        return 0
+    chips_x = min(CHIPS_X, chips)
+    chips_y = chips // chips_x
+    chip_y, chip_x = chip // chips_x, chip % chips_x
+    steps = sorted(
+        [(dy, dx) for dy in range(chips_y) for dx in range(chips_x) if dy or dx],
+        key=lambda s: -(min(s[0], chips_y - s[0]) + min(s[1], chips_x - s[1])),
+    )
+    others = [
+        lax.rem(chip_y + dy, chips_y) * chips_x + lax.rem(chip_x + dx, chips_x) for dy, dx in steps
+    ]
 
     def await_scan(phase):
         all_of = gathered.at[pl.ds(0, chips - 1)]
         pltpu.make_async_copy(all_of, all_of, scan_sems.at[2 * phase]).wait()
         pltpu.make_async_copy(all_of, all_of, scan_sems.at[2 * phase + 1]).wait()
 
-    lax.fori_loop(1, chips, scatter, 0)
+    for to in others:
+        scan_copy(chip_sum.at[scan_rows(to)], gathered.at[chip], 0, to).start()
     gathered[chip] = chip_sum[scan_rows(chip), :]
 
     def scoring(h, _):
@@ -217,19 +230,14 @@
     lax.fori_loop(0, heads, scoring, 0)
     await_scan(0)
 
-    def prefix(i, running):
+    running = jnp.zeros((share, depth), F32)
+    for i in range(chips):
         c = i + core * (chips - 1 - 2 * i)
         prefixes[c] = running
-        return running + gathered[c]
-
-    lax.fori_loop(0, chips, prefix, jnp.zeros((share, depth), F32))
-
-    def give_back(i, _):
-        to = lax.rem(chip + i, chips)
+        running = running + gathered[c]
+
+    for to in others:
         scan_copy(prefixes.at[to], entering.at[scan_rows(chip)], 1, to).start()
-        return 0
-
-    lax.fori_loop(1, chips, give_back, 0)
     entering[scan_rows(chip), :] = prefixes[chip]
 
     def inside(h, _):
@@ -246,35 +254,66 @@
     hand = to_partner(passed, received, 1)
     hand.start()
 
-    def apply(which, state):
-        def body(h, _):
-            held = state[pl.ds(pl.multiple_of(h * depth, depth), depth), :]
+    def each_state(state, body):
+        def at_head(h, _):
+            body(h, state[pl.ds(pl.multiple_of(h * depth, depth), depth), :])
+            return 0
+
+        lax.fori_loop(0, heads, at_head, 0)
+
+    def apply_second(which, state):
+        def body(h, held):
+            second[which, h] += product(other[which, h], held, NT)
+
+        each_state(state, body)
+
+    def apply_first(which, state):
+        def body(h, held):
             first[which, h] += product(unit[which, h], held, NN)
-            second[which, h] += product(other[which, h], held, NT)
-            return 0
-
-        lax.fori_loop(0, heads, body, 0)
-
-    apply(core, entering)
+
+        each_state(state, body)
+
+    apply_second(core, entering)
     hand.wait()
-    apply(1 - core, received)
-
-    query_inner = jnp.zeros((tokens, depth), F32)
-    key_inner = jnp.zeros((tokens, depth), F32)
+    apply_second(1 - core, received)
+
+    inner = [jnp.zeros((tokens, depth), F32) for _ in range(2)]
     for h in range(heads):
-        query_inner += unit[0, h] * second[0, h]
-        key_inner += unit[1, h] * second[1, h]
-    share_sums(1, query_inner, key_inner)
+        for i in range(2):
+            inner[i] += unit[i, h] * second[i, h]
+    share_sums(1, *inner)
     send_shares(1)
+
+    apply_first(core, entering)
+    apply_first(1 - core, received)
     for h in range(heads):
         att_ref[rows_of(h), :] = first[0, h] * weight[...]
         gv_ref[rows_of(h), :] = first[1, h]
+    for i in range(2):
+        for h in range(heads):
+            second[i, h] = second[i, h] * gains[i, pl.ds(h, 1), :] * scales[i]
+            other[i, h] = raw[i, rows_of(h), :] * (scales[i] * scales[i])
     mean = await_shares(1) / width
-    for i, (gain, out) in enumerate(((q_gain, gq_ref), (k_gain, gk_ref))):
-        along = down_rows(mean, i) * scales[i]
+    for i, out in enumerate((gq_ref, gk_ref)):
+        along = down_rows(mean, i)
         for h in range(heads):
-            push = second[i, h] * gain[pl.ds(h, 1), :]
-            out[rows_of(h), :] = scales[i] * (push - raw[i, rows_of(h), :] * along)
+            out[rows_of(h), :] = second[i, h] - other[i, h] * along
+
+
+def leave(*refs):
+    sources, targets, sems = refs[:4], refs[4:8], refs[8]
+    copies = [
+        pltpu.make_async_copy(src, dst, sems.at[i])
+        for i, (src, dst) in enumerate(zip(sources, targets))
+    ]
+    for copy in copies:
+        copy.start()
+    for copy in copies:
+        copy.wait()
+
+
+def kept(x):
+    return pltpu.with_memory_space_constraint(x, pltpu.HBM)
 
 
 def local(n_seq, n_head, query_raw, key_raw, value_raw, query_gain, key_gain, cotangent):
@@ -283,15 +322,16 @@
     flat = (tokens * heads, depth)
     states = (heads * depth, depth)
     per_owner = (chips, heads * depth // chips, depth)
-    anywhere = pl.BlockSpec(memory_space=pl.ANY)
+    hbm = pl.BlockSpec(memory_space=pltpu.HBM)
     vmem = pl.BlockSpec(memory_space=pltpu.VMEM)
     outs = pl.pallas_call(
         functools.partial(kernel, n_seq, n_head, heads, tokens, depth),
         out_shape=[jax.ShapeDtypeStruct(flat, F32)] * 4,
-        in_specs=[anywhere] * 4 + [vmem] * 2,
+        in_specs=[hbm] * 6,
         out_specs=[vmem] * 4,
         scratch_shapes=[
             pltpu.VMEM((4, *flat), F32),
+            pltpu.VMEM((2, heads, depth), F32),
             pltpu.VMEM((2, heads, tokens, depth), F32),
             pltpu.VMEM((2, heads, tokens, depth), F32),
             pltpu.VMEM((2, heads, tokens, depth), F32),
@@ -310,7 +350,7 @@
             pltpu.VMEM(states, F32),
             pltpu.VMEM(states, F32),
             pltpu.VMEM(states, F32),
-            pltpu.SemaphoreType.DMA((4,)),
+            pltpu.SemaphoreType.DMA((6,)),
             pltpu.SemaphoreType.DMA((4,)),
             pltpu.SemaphoreType.DMA((4,)),
             pltpu.SemaphoreType.DMA((4,)),
@@ -319,10 +359,18 @@
             collective_id=0, has_side_effects=True, vmem_limit_bytes=48 * 1024 * 1024
         ),
     )(
-        *(x.reshape(flat) for x in (query_raw, key_raw, value_raw, cotangent)),
-        query_gain,
-        key_gain,
+        *(kept(x.reshape(flat)) for x in (query_raw, key_raw, value_raw, cotangent)),
+        kept(query_gain),
+        kept(key_gain),
     )
+    outs = pl.pallas_call(
+        leave,
+        out_shape=[jax.ShapeDtypeStruct(flat, F32)] * 4,
+        in_specs=[vmem] * 4,
+        out_specs=[hbm] * 4,
+        scratch_shapes=[pltpu.SemaphoreType.DMA((4,))],
+        compiler_params=pltpu.CompilerParams(vmem_limit_bytes=4 * 1024 * 1024),
+    )(*outs)
     return tuple(x.reshape(tokens, heads, depth) for x in outs)
 
 

time: 65.5 us -> 56.8 us (0.87)
  local copies, waits for them, and re-layouts: 8.02 us -> 0 us
    unnamed x16 -> x0, local copies, waits for them, and re-layouts: 8.02 us -> none
    pallas_call x1, Pallas kernels: 56.4 us -> 54.6 us  [local(): pl.pallas_call(functools.partial(kernel, n_seq, n_head, heads, tokens, de...]
    pallas_call x0 -> x1, Pallas kernels: none -> 1.35 us  [local(): pl.pallas_call(leave, out_shape=[jax.ShapeDtypeStruct(flat, F32)] * 4, in...]
where the time goes in v2:
time: 56.8 us; the launch traced here: 56.6 us
  Pallas kernels  56 us (99%)
  between operations  0.64 us (1%)
    pallas_call x1, Pallas kernels, local(): pl.pallas_call(functools.partial(kernel, n_seq, n_head, heads, tokens, de...  54.6 us
    pallas_call x1, Pallas kernels, local(): pl.pallas_call(leave, out_shape=[jax.ShapeDtypeStruct(flat, F32)] * 4, in...  1.35 us

profile of v2, /device:TPU:1, one launch (start us, length us, event | category | flops | bytes accessed | tf_op | source)
XLA Modules:
  0.0 56.6 jit_solution(3166222367034736404)
XLA Ops:
  0.6 54.6 %shard_map.93 = (f32[1024,128]{1,0:T(8,128)S(1)}, f32[1024,128]{1,0:T(8,128)S(1)}, f32[1024,128]{1,0:T(8,128)S(1)}, f32[1024,128]{1,0:T(8,128)S(1)}) custom-call(f32[1024,128]{1,0:T(8,128)} %bitcast.8, f32[1024,128]{1,0:T(8,128)} %bitcast.9, f32[1024,128]{1,0:T(8,128)} %bitcast.10, f32[1024,128]{1,0:T(8,128)} %bitcast.11, f32[4,128]{1,0:T(4,128)} %q_gain_hbm.1, ...), custom_call_target="tpu_custom_call" | custom-call | tf_op jit(solution)/shard_map/pallas_call | solution.py:327
  55.3 1.3 %shard_map.94 = (f32[1024,128]{1,0:T(8,128)}, f32[1024,128]{1,0:T(8,128)}, f32[1024,128]{1,0:T(8,128)}, f32[1024,128]{1,0:T(8,128)}) custom-call(f32[1024,128]{1,0:T(8,128)S(1)} %get-tuple-element.12.refs_0_, f32[1024,128]{1,0:T(8,128)S(1)} %get-tuple-element.13.refs_1_, f32[1024,128]{1,0:T(8,128)S(1)} %get-tuple-element.14.refs_2_, ...), custom_call_target="tpu_custom_call" | custom-call | tf_op jit(solution)/shard_map/pallas_call | solution.py:366

commit v3 on v2

--- a/solution.py
+++ b/solution.py
@@ -22,12 +22,22 @@
     return high, (x - high.astype(F32)).astype(BF16)
 
 
+def left_parts(x, axis):
+    high, low = halves(x)
+    return jnp.concatenate([high, low, high], axis=axis)
+
+
+def right_parts(x, axis):
+    high, low = halves(x)
+    return jnp.concatenate([high, high, low], axis=axis)
+
+
+def dot(left, right, form):
+    return lax.dot_general(left, right, (form, ((), ())), preferred_element_type=F32)
+
+
 def product(left, right, form):
-    left_high, left_low = halves(left)
-    right_high, right_low = halves(right)
-    left_parts = jnp.concatenate([left_high, left_low, left_high], axis=form[0][0])
-    right_parts = jnp.concatenate([right_high, right_high, right_low], axis=form[1][0])
-    return lax.dot_general(left_parts, right_parts, (form, ((), ())), preferred_element_type=F32)
+    return dot(left_parts(left, form[0][0]), right_parts(right, form[1][0]), form)
 
 
 def lane_sums(x):
@@ -35,14 +45,24 @@
     rest = (x - high.astype(F32) - low.astype(F32)).astype(BF16)
     parts = jnp.concatenate([high, low, rest], axis=1)
     ones = jnp.ones((8, parts.shape[1]), BF16)
-    return lax.dot_general(ones, parts, (NT, ((), ())), preferred_element_type=F32)
+    return dot(ones, parts, NT)
+
+
+def down_rows(line, i, tokens):
+    return jnp.concatenate(
+        [
+            jnp.broadcast_to(line[2 * i + j : 2 * i + j + 1, :], (128, 128)).T
+            for j in range(tokens // 128)
+        ],
+        axis=0,
+    )
 
 
 def kernel(
     n_seq, n_head, heads, tokens, depth,
     q_hbm, k_hbm, v_hbm, c_hbm, q_gain_hbm, k_gain_hbm,
-    att_ref, gq_ref, gk_ref, gv_ref,
-    raw, gains, unit, other, first, second, mix, score, weight, scales,
+    att_ref, gv_ref, push_ref, base_ref, mean_ref,
+    raw, gains, unit, other, turned, split, first, second, mix, score, weight, scales,
     z_send, z_recv, states, peer, chip_sum, gathered, prefixes, entering, passed, received,
     load_sem, z_sems, core_sems, scan_sems,
 ):
@@ -111,18 +131,8 @@
 
     def await_shares(slot):
         all_of = z_recv.at[slot, pl.ds(0, n_head - 1)]
-        pltpu.make_async_copy(all_of, all_of, z_sems.at[2 * slot]).wait()
         pltpu.make_async_copy(all_of, all_of, z_sems.at[2 * slot + 1]).wait()
         return jnp.sum(z_recv[slot], axis=0)
-
-    def down_rows(line, i):
-        return jnp.concatenate(
-            [
-                jnp.broadcast_to(line[2 * i + j : 2 * i + j + 1, :], (128, 128)).T
-                for j in range(tokens // 128)
-            ],
-            axis=0,
-        )
 
     loads[0].wait()
     loads[1].wait()
@@ -146,6 +156,17 @@
     for h in range(heads):
         other[0, h] = raw[3, rows_of(h), :] * weight[...]
         other[1, h] = raw[2, rows_of(h), :]
+    for i in range(2):
+        for h in range(heads):
+            unit[i, h] = raw[i, rows_of(h), :] * gains[i, pl.ds(h, 1), :]
+
+    def turning(h, _):
+        for i in range(2):
+            turned[i, h] = left_parts(other[i, h].T, 1)
+            split[i, h] = left_parts(other[i, h], 1)
+        return 0
+
+    lax.fori_loop(0, heads, turning, 0)
 
     rows = lax.broadcasted_iota(jnp.int32, (tokens, tokens), 0)
     columns = lax.broadcasted_iota(jnp.int32, (tokens, tokens), 1)
@@ -160,35 +181,35 @@
     total = await_shares(0)
     scale = lax.rsqrt(total / width + EPSILON)
     for i in range(2):
-        scales[i] = down_rows(scale, i)
-    for i in range(2):
-        for h in range(heads):
-            unit[i, h] = raw[i, rows_of(h), :] * scales[i] * gains[i, pl.ds(h, 1), :]
-
-    def block_states(which):
-        def body(h, _):
-            at = pl.ds(pl.multiple_of(h * depth, depth), depth)
-            states[which, at, :] = product(unit[1 - which, h], other[1 - which, h], TN)
-            return 0
-
-        lax.fori_loop(0, heads, body, 0)
-
-    def to_partner(src, dst, i):
+        scales[i] = down_rows(scale, i, tokens)
+
+    def at_head(h):
+        return pl.ds(h * depth, depth)
+
+    def block_state(which, h):
+        normed = unit[1 - which, h] * scales[1 - which]
+        unit[1 - which, h] = normed
+        states[which, at_head(h), :] = dot(turned[1 - which, h], right_parts(normed, 0), NN)
+
+    def to_partner(src, dst, phase, h):
         return pltpu.make_async_remote_copy(
-            src_ref=src,
-            dst_ref=dst,
-            send_sem=core_sems.at[2 * i],
-            recv_sem=core_sems.at[2 * i + 1],
+            src_ref=src.at[at_head(h)],
+            dst_ref=dst.at[at_head(h)],
+            send_sem=core_sems.at[phase, 0, h],
+            recv_sem=core_sems.at[phase, 1, h],
             device_id=partner,
             device_id_type=MESH,
         )
 
-    block_states(1 - core)
-    swap = to_partner(states.at[1 - core], peer, 0)
-    swap.start()
-    block_states(core)
-    swap.wait()
-    chip_sum[...] = states[core] + peer[...]
+    swaps = [to_partner(states.at[1 - core], peer, 0, h) for h in range(heads)]
+    for h in range(heads):
+        block_state(1 - core, h)
+        swaps[h].start()
+    for h in range(heads):
+        block_state(core, h)
+    for h in range(heads):
+        swaps[h].wait_recv()
+        chip_sum[at_head(h), :] = states[core, at_head(h), :] + peer[at_head(h), :]
 
     def scan_rows(c):
         return pl.ds(pl.multiple_of(c * share, share), share)
@@ -216,7 +237,6 @@
 
     def await_scan(phase):
         all_of = gathered.at[pl.ds(0, chips - 1)]
-        pltpu.make_async_copy(all_of, all_of, scan_sems.at[2 * phase]).wait()
         pltpu.make_async_copy(all_of, all_of, scan_sems.at[2 * phase + 1]).wait()
 
     for to in others:
@@ -250,32 +270,27 @@
     lax.fori_loop(0, heads, inside, 0)
     await_scan(1)
 
-    passed[...] = entering[...] + states[core]
-    hand = to_partner(passed, received, 1)
-    hand.start()
-
-    def each_state(state, body):
-        def at_head(h, _):
-            body(h, state[pl.ds(pl.multiple_of(h * depth, depth), depth), :])
+    hands = [to_partner(passed, received, 1, h) for h in range(heads)]
+    for h in range(heads):
+        passed[at_head(h), :] = entering[at_head(h), :] + states[core, at_head(h), :]
+        hands[h].start()
+
+    def apply_second(which, state, h):
+        second[which, h] += dot(split[which, h], right_parts(state[at_head(h), :], 0), NN)
+
+    def apply_first(which, state):
+        def body(h, _):
+            held = state[pl.ds(pl.multiple_of(h * depth, depth), depth), :]
+            first[which, h] += product(unit[which, h], held, NT)
             return 0
 
-        lax.fori_loop(0, heads, at_head, 0)
-
-    def apply_second(which, state):
-        def body(h, held):
-            second[which, h] += product(other[which, h], held, NT)
-
-        each_state(state, body)
-
-    def apply_first(which, state):
-        def body(h, held):
-            first[which, h] += product(unit[which, h], held, NN)
-
-        each_state(state, body)
-
-    apply_second(core, entering)
-    hand.wait()
-    apply_second(1 - core, received)
+        lax.fori_loop(0, heads, body, 0)
+
+    for h in range(heads):
+        apply_second(core, entering, h)
+    for h in range(heads):
+        hands[h].wait_recv()
+        apply_second(1 - core, received, h)
 
     inner = [jnp.zeros((tokens, depth), F32) for _ in range(2)]
     for h in range(heads):
@@ -291,23 +306,40 @@
         gv_ref[rows_of(h), :] = first[1, h]
     for i in range(2):
         for h in range(heads):
-            second[i, h] = second[i, h] * gains[i, pl.ds(h, 1), :] * scales[i]
-            other[i, h] = raw[i, rows_of(h), :] * (scales[i] * scales[i])
-    mean = await_shares(1) / width
-    for i, out in enumerate((gq_ref, gk_ref)):
-        along = down_rows(mean, i)
-        for h in range(heads):
-            out[rows_of(h), :] = second[i, h] - other[i, h] * along
-
-
-def leave(*refs):
-    sources, targets, sems = refs[:4], refs[4:8], refs[8]
+            push_ref[i, h] = second[i, h] * gains[i, pl.ds(h, 1), :] * scales[i]
+            base_ref[i, h] = raw[i, rows_of(h), :] * (scales[i] * scales[i])
+    mean_ref[...] = await_shares(1) / width
+
+    for h in range(heads):
+        swaps[h].wait_send()
+        hands[h].wait_send()
+    for slot in range(2):
+        all_of = z_recv.at[slot, pl.ds(0, n_head - 1)]
+        pltpu.make_async_copy(all_of, all_of, z_sems.at[2 * slot]).wait()
+    for phase in range(2):
+        all_of = gathered.at[pl.ds(0, chips - 1)]
+        pltpu.make_async_copy(all_of, all_of, scan_sems.at[2 * phase]).wait()
+
+
+def leave(
+    heads, tokens, att_ref, gv_ref, push_ref, base_ref, mean_ref,
+    att_out, gq_out, gk_out, gv_out, staged, sems,
+):
     copies = [
         pltpu.make_async_copy(src, dst, sems.at[i])
-        for i, (src, dst) in enumerate(zip(sources, targets))
+        for i, (src, dst) in enumerate(
+            ((att_ref, att_out), (gv_ref, gv_out), (staged.at[0], gq_out), (staged.at[1], gk_out))
+        )
     ]
-    for copy in copies:
-        copy.start()
+    copies[0].start()
+    copies[1].start()
+    mean = mean_ref[...]
+    for i in range(2):
+        along = down_rows(mean, i, tokens)
+        for h in range(heads):
+            rows = pl.ds(h, tokens, stride=heads)
+            staged[i, rows, :] = push_ref[i, h] - base_ref[i, h] * along
+        copies[2 + i].start()
     for copy in copies:
         copy.wait()
 
@@ -320,22 +352,28 @@
     tokens, heads, depth = query_raw.shape
     chips = n_seq // 2
     flat = (tokens * heads, depth)
+    both = (2, heads, tokens, depth)
     states = (heads * depth, depth)
     per_owner = (chips, heads * depth // chips, depth)
     hbm = pl.BlockSpec(memory_space=pltpu.HBM)
     vmem = pl.BlockSpec(memory_space=pltpu.VMEM)
     outs = pl.pallas_call(
         functools.partial(kernel, n_seq, n_head, heads, tokens, depth),
-        out_shape=[jax.ShapeDtypeStruct(flat, F32)] * 4,
+        out_shape=[
+            jax.ShapeDtypeStruct(shape, F32)
+            for shape in (flat, flat, both, both, (2 * tokens // 128, 128))
+        ],
         in_specs=[hbm] * 6,
-        out_specs=[vmem] * 4,
+        out_specs=[vmem] * 5,
         scratch_shapes=[
             pltpu.VMEM((4, *flat), F32),
             pltpu.VMEM((2, heads, depth), F32),
-            pltpu.VMEM((2, heads, tokens, depth), F32),
-            pltpu.VMEM((2, heads, tokens, depth), F32),
-            pltpu.VMEM((2, heads, tokens, depth), F32),
-            pltpu.VMEM((2, heads, tokens, depth), F32),
+            pltpu.VMEM(both, F32),
+            pltpu.VMEM(both, F32),
+            pltpu.VMEM((2, heads, depth, 3 * tokens), BF16),
+            pltpu.VMEM((2, heads, tokens, 3 * depth), BF16),
+            pltpu.VMEM(both, F32),
+            pltpu.VMEM(both, F32),
             pltpu.VMEM((heads, tokens, tokens), F32),
             pltpu.VMEM((heads, tokens, tokens), F32),
             pltpu.VMEM((tokens, depth), F32),
@@ -352,7 +390,7 @@
             pltpu.VMEM(states, F32),
             pltpu.SemaphoreType.DMA((6,)),
             pltpu.SemaphoreType.DMA((4,)),
-            pltpu.SemaphoreType.DMA((4,)),
+            pltpu.SemaphoreType.DMA((2, 2, heads)),
             pltpu.SemaphoreType.DMA((4,)),
         ],
         compiler_params=pltpu.CompilerParams(
@@ -364,11 +402,11 @@
         kept(key_gain),
     )
     outs = pl.pallas_call(
-        leave,
+        functools.partial(leave, heads, tokens),
         out_shape=[jax.ShapeDtypeStruct(flat, F32)] * 4,
-        in_specs=[vmem] * 4,
+        in_specs=[vmem] * 5,
         out_specs=[hbm] * 4,
-        scratch_shapes=[pltpu.SemaphoreType.DMA((4,))],
+        scratch_shapes=[pltpu.VMEM((2, *flat), F32), pltpu.SemaphoreType.DMA((4,))],
         compiler_params=pltpu.CompilerParams(vmem_limit_bytes=4 * 1024 * 1024),
     )(*outs)
     return tuple(x.reshape(tokens, heads, depth) for x in outs)

time: 56.8 us -> 56.2 us (0.989)
  Pallas kernels: 56 us -> 55.4 us
where the time goes in v3:
time: 56.2 us; the launch traced here: 56.1 us
  Pallas kernels  55.4 us (99%)
  between operations  0.64 us (1%)
    pallas_call x1, Pallas kernels, local(): pl.pallas_call(functools.partial(kernel, n_seq, n_head, heads, tokens, de...  54.1 us
    pallas_call x1, Pallas kernels, local(): pl.pallas_call(functools.partial(leave, heads, tokens), out_shape=[jax.Sh...  1.35 us

profile of v3, /device:TPU:1, one launch (start us, length us, event | category | flops | bytes accessed | tf_op | source)
XLA Modules:
  0.0 56.1 jit_solution(11219437067873385243)
XLA Ops:
  0.6 54.1 %shard_map.93 = (f32[1024,128]{1,0:T(8,128)S(1)}, f32[1024,128]{1,0:T(8,128)S(1)}, f32[2,4,256,128]{3,2,1,0:T(8,128)S(1)}, f32[2,4,256,128]{3,2,1,0:T(8,128)S(1)}, f32[4,128]{1,0:T(4,128)S(1)}) custom-call(f32[1024,128]{1,0:T(8,128)} %bitcast.8, f32[1024,128]{1,0:T(8,128)} %bitcast.9, f32[1024,128]{1,0:T(8,128)} %bitcast.10, f32[1024,128]{1,0:T(8,128)} %bitcast.11, ...), custom_call_target="tpu_custom_call" | custom-call | tf_op jit(solution)/shard_map/pallas_call | solution.py:360
  54.7 1.3 %shard_map.94 = (f32[1024,128]{1,0:T(8,128)}, f32[1024,128]{1,0:T(8,128)}, f32[1024,128]{1,0:T(8,128)}, f32[1024,128]{1,0:T(8,128)}) custom-call(f32[1024,128]{1,0:T(8,128)S(1)} %get-tuple-element.13.att_ref, f32[1024,128]{1,0:T(8,128)S(1)} %get-tuple-element.14.gv_ref, f32[2,4,256,128]{3,2,1,0:T(8,128)S(1)} %get-tuple-element.15.push_ref, ...), custom_call_target="tpu_custom_call" | custom-call | tf_op jit(solution)/shard_map/pallas_call | solution.py:404

commit v4 on v3

--- a/solution.py
+++ b/solution.py
@@ -63,8 +63,10 @@
     q_hbm, k_hbm, v_hbm, c_hbm, q_gain_hbm, k_gain_hbm,
     att_ref, gv_ref, push_ref, base_ref, mean_ref,
     raw, gains, unit, other, turned, split, first, second, mix, score, weight, scales,
-    z_send, z_recv, states, peer, chip_sum, gathered, prefixes, entering, passed, received,
-    load_sem, z_sems, core_sems, scan_sems,
+    z_send, z_recv, part_send, part_recv, line_scale, staged_unit, peer_unit, peer_other,
+    peer_split,
+    states, peer, chip_sum, gathered, prefixes, entering, passed, received,
+    load_sem, z_sems, part_sems, push_sems, core_sems, scan_sems,
 ):
     chips = n_seq // 2
     share = heads * depth // chips
@@ -83,146 +85,6 @@
         load.start()
 
     barrier = pltpu.get_barrier_semaphore()
-
-    def greet_head(d, _):
-        pl.semaphore_signal(
-            barrier, inc=1, device_id=(seq, lax.rem(head + d, n_head)), device_id_type=MESH
-        )
-        return 0
-
-    def greet_chip(d, _):
-        to = lax.rem(chip + d, chips)
-        pl.semaphore_signal(barrier, inc=1, device_id=(2 * to + core, head), device_id_type=MESH)
-        return 0
-
-    lax.fori_loop(1, n_head, greet_head, 0)
-    lax.fori_loop(1, chips, greet_chip, 0)
-    partner = (2 * chip + 1 - core, head)
-    pl.semaphore_signal(barrier, inc=1, device_id=partner, device_id_type=MESH)
-
-    def rows_of(h):
-        return pl.ds(h, tokens, stride=heads)
-
-    def share_sums(slot, of_query, of_key):
-        send, recv = z_send.at[slot], z_recv.at[slot]
-        for i, of_one in enumerate((of_query, of_key)):
-            sums = lane_sums(of_one)
-            for j in range(tokens // 128):
-                send[pl.ds(2 * i + j, 1), :] = sums[0:1, 128 * j : 128 * (j + 1)]
-        recv[head] = send[...]
-
-    def share_copy(slot, d):
-        return pltpu.make_async_remote_copy(
-            src_ref=z_send.at[slot],
-            dst_ref=z_recv.at[slot, head],
-            send_sem=z_sems.at[2 * slot],
-            recv_sem=z_sems.at[2 * slot + 1],
-            device_id=(seq, lax.rem(head + d, n_head)),
-            device_id_type=MESH,
-        )
-
-    def send_shares(slot):
-        def body(i, _):
-            step = (i + 1) // 2
-            share_copy(slot, n_head // 2 + step * (1 - 2 * (i % 2))).start()
-            return 0
-
-        lax.fori_loop(0, n_head - 1, body, 0)
-
-    def await_shares(slot):
-        all_of = z_recv.at[slot, pl.ds(0, n_head - 1)]
-        pltpu.make_async_copy(all_of, all_of, z_sems.at[2 * slot + 1]).wait()
-        return jnp.sum(z_recv[slot], axis=0)
-
-    loads[0].wait()
-    loads[1].wait()
-    query_squares = jnp.zeros((tokens, depth), F32)
-    key_squares = jnp.zeros((tokens, depth), F32)
-    for h in range(heads):
-        q, k = raw[0, rows_of(h), :], raw[1, rows_of(h), :]
-        query_squares += q * q
-        key_squares += k * k
-    share_sums(0, query_squares, key_squares)
-
-    pl.semaphore_wait(barrier, n_head - 1 + chips - 1 + 1)
-    send_shares(0)
-
-    loads[2].wait()
-    loads[3].wait()
-    loads[4].wait()
-    loads[5].wait()
-    position = (seq * tokens + lax.broadcasted_iota(jnp.int32, (tokens, depth), 0)).astype(F32)
-    weight[...] = lax.rsqrt(float(depth) * (position + 1.0))
-    for h in range(heads):
-        other[0, h] = raw[3, rows_of(h), :] * weight[...]
-        other[1, h] = raw[2, rows_of(h), :]
-    for i in range(2):
-        for h in range(heads):
-            unit[i, h] = raw[i, rows_of(h), :] * gains[i, pl.ds(h, 1), :]
-
-    def turning(h, _):
-        for i in range(2):
-            turned[i, h] = left_parts(other[i, h].T, 1)
-            split[i, h] = left_parts(other[i, h], 1)
-        return 0
-
-    lax.fori_loop(0, heads, turning, 0)
-
-    rows = lax.broadcasted_iota(jnp.int32, (tokens, tokens), 0)
-    columns = lax.broadcasted_iota(jnp.int32, (tokens, tokens), 1)
-    causal = rows >= columns
-
-    def mixing(h, _):
-        mix[h] = jnp.where(causal, product(other[0, h], other[1, h], NT), 0.0)
-        return 0
-
-    lax.fori_loop(0, heads, mixing, 0)
-
-    total = await_shares(0)
-    scale = lax.rsqrt(total / width + EPSILON)
-    for i in range(2):
-        scales[i] = down_rows(scale, i, tokens)
-
-    def at_head(h):
-        return pl.ds(h * depth, depth)
-
-    def block_state(which, h):
-        normed = unit[1 - which, h] * scales[1 - which]
-        unit[1 - which, h] = normed
-        states[which, at_head(h), :] = dot(turned[1 - which, h], right_parts(normed, 0), NN)
-
-    def to_partner(src, dst, phase, h):
-        return pltpu.make_async_remote_copy(
-            src_ref=src.at[at_head(h)],
-            dst_ref=dst.at[at_head(h)],
-            send_sem=core_sems.at[phase, 0, h],
-            recv_sem=core_sems.at[phase, 1, h],
-            device_id=partner,
-            device_id_type=MESH,
-        )
-
-    swaps = [to_partner(states.at[1 - core], peer, 0, h) for h in range(heads)]
-    for h in range(heads):
-        block_state(1 - core, h)
-        swaps[h].start()
-    for h in range(heads):
-        block_state(core, h)
-    for h in range(heads):
-        swaps[h].wait_recv()
-        chip_sum[at_head(h), :] = states[core, at_head(h), :] + peer[at_head(h), :]
-
-    def scan_rows(c):
-        return pl.ds(pl.multiple_of(c * share, share), share)
-
-    def scan_copy(src, dst, phase, to):
-        return pltpu.make_async_remote_copy(
-            src_ref=src,
-            dst_ref=dst,
-            send_sem=scan_sems.at[2 * phase],
-            recv_sem=scan_sems.at[2 * phase + 1],
-            device_id=(2 * to + core, head),
-            device_id_type=MESH,
-        )
 
     chips_x = min(CHIPS_X, chips)
     chips_y = chips // chips_x
@@ -234,6 +96,165 @@
     others = [
         lax.rem(chip_y + dy, chips_y) * chips_x + lax.rem(chip_x + dx, chips_x) for dy, dx in steps
     ]
+    heads_on = [
+        lax.rem(head + d, n_head)
+        for d in sorted(range(1, n_head), key=lambda d: -min(d, n_head - d))
+    ]
+    peer_seq = 2 * chip + 1 - core
+    partner = (peer_seq, head)
+    greeted = [(seq, to) for to in heads_on] + [(2 * to + core, head) for to in others]
+    greeted += [(peer_seq, to) for to in heads_on] + [partner]
+    for device in greeted:
+        pl.semaphore_signal(barrier, inc=1, device_id=device, device_id_type=MESH)
+
+    def rows_of(h):
+        return pl.ds(h, tokens, stride=heads)
+
+    def share_sums(slot, of_query, of_key):
+        send, recv = z_send.at[slot], z_recv.at[slot]
+        for i, of_one in enumerate((of_query, of_key)):
+            sums = lane_sums(of_one)
+            for j in range(tokens // 128):
+                send[pl.ds(2 * i + j, 1), :] = sums[0:1, 128 * j : 128 * (j + 1)]
+        recv[head] = send[...]
+
+    def share_copy(slot, to):
+        return pltpu.make_async_remote_copy(
+            src_ref=z_send.at[slot],
+            dst_ref=z_recv.at[slot, head],
+            send_sem=z_sems.at[2 * slot],
+            recv_sem=z_sems.at[2 * slot + 1],
+            device_id=(seq, to),
+            device_id_type=MESH,
+        )
+
+    def send_shares(slot):
+        for to in heads_on:
+            share_copy(slot, to).start()
+
+    def part_copy(kind, device):
+        return pltpu.make_async_remote_copy(
+            src_ref=part_send.at[kind],
+            dst_ref=part_recv.at[kind, head],
+            send_sem=part_sems.at[2 * kind],
+            recv_sem=part_sems.at[2 * kind + 1],
+            device_id=device,
+            device_id_type=MESH,
+        )
+
+    def await_shares(slot):
+        all_of = z_recv.at[slot, pl.ds(0, n_head - 1)]
+        pltpu.make_async_copy(all_of, all_of, z_sems.at[2 * slot + 1]).wait()
+        return jnp.sum(z_recv[slot], axis=0)
+
+    loads[0].wait()
+    loads[1].wait()
+    query_squares = jnp.zeros((tokens, depth), F32)
+    key_squares = jnp.zeros((tokens, depth), F32)
+    for h in range(heads):
+        q, k = raw[0, rows_of(h), :], raw[1, rows_of(h), :]
+        query_squares += q * q
+        key_squares += k * k
+    share_sums(0, query_squares, key_squares)
+
+    pl.semaphore_wait(barrier, len(greeted))
+    send_shares(0)
+
+    loads[2].wait()
+    loads[3].wait()
+    loads[4].wait()
+    loads[5].wait()
+    position = (seq * tokens + lax.broadcasted_iota(jnp.int32, (tokens, depth), 0)).astype(F32)
+    weight[...] = lax.rsqrt(float(depth) * (position + 1.0))
+    for h in range(heads):
+        other[0, h] = raw[3, rows_of(h), :] * weight[...]
+        other[1, h] = raw[2, rows_of(h), :]
+    for i in range(2):
+        for h in range(heads):
+            unit[i, h] = raw[i, rows_of(h), :] * gains[i, pl.ds(h, 1), :]
+
+    pushes = [
+        pltpu.make_async_remote_copy(
+            src_ref=src,
+            dst_ref=dst,
+            send_sem=push_sems.at[2 * i],
+            recv_sem=push_sems.at[2 * i + 1],
+            device_id=partner,
+            device_id_type=MESH,
+        )
+        for i, (src, dst) in enumerate(
+            ((other.at[1 - core], peer_other), (staged_unit, peer_unit))
+        )
+    ]
+    for h in range(heads):
+        staged_unit[h] = unit[1 - core, h]
+    for push in pushes:
+        push.start()
+
+    def turning(h, _):
+        for i in range(2):
+            turned[i, h] = left_parts(other[i, h].T, 1)
+            split[i, h] = left_parts(other[i, h], 1)
+        return 0
+
+    lax.fori_loop(0, heads, turning, 0)
+
+    rows = lax.broadcasted_iota(jnp.int32, (tokens, tokens), 0)
+    columns = lax.broadcasted_iota(jnp.int32, (tokens, tokens), 1)
+    causal = rows >= columns
+
+    def mixing(h, _):
+        mix[h] = jnp.where(causal, product(other[0, h], other[1, h], NT), 0.0)
+        return 0
+
+    lax.fori_loop(0, heads, mixing, 0)
+
+    total = await_shares(0)
+    scale = lax.rsqrt(total / width + EPSILON)
+    line_scale[...] = scale
+    for i in range(2):
+        scales[i] = down_rows(scale, i, tokens)
+
+    def at_head(h):
+        return pl.ds(h * depth, depth)
+
+    def block_state(which, h):
+        normed = unit[1 - which, h] * scales[1 - which]
+        unit[1 - which, h] = normed
+        states[which, at_head(h), :] = dot(turned[1 - which, h], right_parts(normed, 0), NN)
+
+    def to_partner(src, dst, phase, h):
+        return pltpu.make_async_remote_copy(
+            src_ref=src.at[at_head(h)],
+            dst_ref=dst.at[at_head(h)],
+            send_sem=core_sems.at[phase, 0, h],
+            recv_sem=core_sems.at[phase, 1, h],
+            device_id=partner,
+            device_id_type=MESH,
+        )
+
+    swaps = [to_partner(states.at[1 - core], peer, 0, h) for h in range(heads)]
+    for h in range(heads):
+        block_state(1 - core, h)
+        swaps[h].start()
+    for h in range(heads):
+        block_state(core, h)
+    for h in range(heads):
+        swaps[h].wait_recv()
+        chip_sum[at_head(h), :] = states[core, at_head(h), :] + peer[at_head(h), :]
+
+    def scan_rows(c):
+        return pl.ds(pl.multiple_of(c * share, share), share)
+
+    def scan_copy(src, dst, phase, to):
+        return pltpu.make_async_remote_copy(
+            src_ref=src,
+            dst_ref=dst,
+            send_sem=scan_sems.at[2 * phase],
+            recv_sem=scan_sems.at[2 * phase + 1],
+            device_id=(2 * to + core, head),
+            device_id_type=MESH,
+        )
 
     def await_scan(phase):
         all_of = gathered.at[pl.ds(0, chips - 1)]
@@ -245,8 +266,11 @@
 
     def scoring(h, _):
         score[h] = jnp.where(causal, product(unit[0, h], unit[1, h], NT), 0.0)
+        peer_split[h] = left_parts(peer_other[h], 1)
         return 0
 
+    for push in pushes:
+        push.wait_recv()
     lax.fori_loop(0, heads, scoring, 0)
     await_scan(0)
 
@@ -268,15 +292,18 @@
         return 0
 
     lax.fori_loop(0, heads, inside, 0)
+    inner = [jnp.zeros((tokens, depth), F32) for _ in range(2)]
+    for h in range(heads):
+        for i in range(2):
+            inner[i] += unit[i, h] * second[i, h]
+    share_sums(1, *inner)
+    send_shares(1)
     await_scan(1)
 
     hands = [to_partner(passed, received, 1, h) for h in range(heads)]
     for h in range(heads):
         passed[at_head(h), :] = entering[at_head(h), :] + states[core, at_head(h), :]
         hands[h].start()
-
-    def apply_second(which, state, h):
-        second[which, h] += dot(split[which, h], right_parts(state[at_head(h), :], 0), NN)
 
     def apply_first(which, state):
         def body(h, _):
@@ -286,19 +313,28 @@
 
         lax.fori_loop(0, heads, body, 0)
 
-    for h in range(heads):
-        apply_second(core, entering, h)
+    own_inner = jnp.zeros((tokens, depth), F32)
+    peer_inner = jnp.zeros((tokens, depth), F32)
+    for h in range(heads):
+        pushed = dot(split[core, h], right_parts(entering[at_head(h), :], 0), NN)
+        second[core, h] += pushed
+        own_inner += unit[core, h] * pushed
+        peer_inner += peer_unit[h] * dot(peer_split[h], right_parts(passed[at_head(h), :], 0), NN)
+    for kind, of_one in enumerate((own_inner, peer_inner)):
+        sums = lane_sums(of_one)
+        for j in range(tokens // 128):
+            part_send[kind, pl.ds(j, 1), :] = sums[0:1, 128 * j : 128 * (j + 1)]
+    for to in heads_on:
+        part_copy(0, (seq, to)).start()
+        part_copy(1, (peer_seq, to)).start()
+    part_copy(1, partner).start()
+    part_recv[0, head] = part_send[0]
+
     for h in range(heads):
         hands[h].wait_recv()
-        apply_second(1 - core, received, h)
-
-    inner = [jnp.zeros((tokens, depth), F32) for _ in range(2)]
-    for h in range(heads):
-        for i in range(2):
-            inner[i] += unit[i, h] * second[i, h]
-    share_sums(1, *inner)
-    send_shares(1)
-
+        second[1 - core, h] += dot(
+            split[1 - core, h], right_parts(received[at_head(h), :], 0), NN
+        )
     apply_first(core, entering)
     apply_first(1 - core, received)
     for h in range(heads):
@@ -308,11 +344,25 @@
         for h in range(heads):
             push_ref[i, h] = second[i, h] * gains[i, pl.ds(h, 1), :] * scales[i]
             base_ref[i, h] = raw[i, rows_of(h), :] * (scales[i] * scales[i])
-    mean_ref[...] = await_shares(1) / width
+    inside_total = await_shares(1)
+    others_here = part_recv.at[0, pl.ds(0, n_head - 1)]
+    pltpu.make_async_copy(others_here, others_here, part_sems.at[1]).wait()
+    pltpu.make_async_copy(part_recv.at[1], part_recv.at[1], part_sems.at[3]).wait()
+    own_part = jnp.sum(part_recv[0], axis=0)
+    peer_part = jnp.sum(part_recv[1], axis=0)
+    pairs = tokens // 128
+    for i in range(2):
+        rows = slice(pairs * i, pairs * (i + 1))
+        part = jnp.where(core == i, own_part, peer_part * line_scale[rows, :])
+        mean_ref[rows, :] = (inside_total[rows, :] + part) / width
 
     for h in range(heads):
         swaps[h].wait_send()
         hands[h].wait_send()
+    for push in pushes:
+        push.wait_send()
+    pltpu.make_async_copy(others_here, others_here, part_sems.at[0]).wait()
+    pltpu.make_async_copy(part_recv.at[1], part_recv.at[1], part_sems.at[2]).wait()
     for slot in range(2):
         all_of = z_recv.at[slot, pl.ds(0, n_head - 1)]
         pltpu.make_async_copy(all_of, all_of, z_sems.at[2 * slot]).wait()
@@ -380,6 +430,13 @@
             pltpu.VMEM((2, tokens, depth), F32),
             pltpu.VMEM((2, 2 * tokens // 128, 128), F32),
             pltpu.VMEM((2, n_head, 2 * tokens // 128, 128), F32),
+            pltpu.VMEM((2, tokens // 128, 128), F32),
+            pltpu.VMEM((2, n_head, tokens // 128, 128), F32),
+            pltpu.VMEM((2 * tokens // 128, 128), F32),
+            pltpu.VMEM(both[1:], F32),
+            pltpu.VMEM(both[1:], F32),
+            pltpu.VMEM(both[1:], F32),
+            pltpu.VMEM((heads, tokens, 3 * depth), BF16),
             pltpu.VMEM((2, *states), F32),
             pltpu.VMEM(states, F32),
             pltpu.VMEM(states, F32),
@@ -389,6 +446,8 @@
             pltpu.VMEM(states, F32),
             pltpu.VMEM(states, F32),
             pltpu.SemaphoreType.DMA((6,)),
+            pltpu.SemaphoreType.DMA((4,)),
+            pltpu.SemaphoreType.DMA((4,)),
             pltpu.SemaphoreType.DMA((4,)),
             pltpu.SemaphoreType.DMA((2, 2, heads)),
             pltpu.SemaphoreType.DMA((4,)),

time: 56.2 us -> 55.3 us (0.984)
  Pallas kernels: 55.4 us -> 54.5 us
    pallas_call x1, Pallas kernels: 54.1 us -> 53.2 us  [local(): pl.pallas_call(functools.partial(kernel, n_seq, n_head, heads, tokens, de...]
where the time goes in v4:
time: 55.3 us; the launch traced here: 55.2 us
  Pallas kernels  54.5 us (99%)
  between operations  0.64 us (1%)
    pallas_call x1, Pallas kernels, local(): pl.pallas_call(functools.partial(kernel, n_seq, n_head, heads, tokens, de...  53.2 us
    pallas_call x1, Pallas kernels, local(): pl.pallas_call(functools.partial(leave, heads, tokens), out_shape=[jax.Sh...  1.35 us

profile of v4, /device:TPU:1, one launch (start us, length us, event | category | flops | bytes accessed | tf_op | source)
XLA Modules:
  0.0 55.2 jit_solution(11900470808174072751)
XLA Ops:
  0.6 53.2 %shard_map.93 = (f32[1024,128]{1,0:T(8,128)S(1)}, f32[1024,128]{1,0:T(8,128)S(1)}, f32[2,4,256,128]{3,2,1,0:T(8,128)S(1)}, f32[2,4,256,128]{3,2,1,0:T(8,128)S(1)}, f32[4,128]{1,0:T(4,128)S(1)}) custom-call(f32[1024,128]{1,0:T(8,128)} %bitcast.8, f32[1024,128]{1,0:T(8,128)} %bitcast.9, f32[1024,128]{1,0:T(8,128)} %bitcast.10, f32[1024,128]{1,0:T(8,128)} %bitcast.11, ...), custom_call_target="tpu_custom_call" | custom-call | tf_op jit(solution)/shard_map/pallas_call | solution.py:410
  53.8 1.3 %shard_map.94 = (f32[1024,128]{1,0:T(8,128)}, f32[1024,128]{1,0:T(8,128)}, f32[1024,128]{1,0:T(8,128)}, f32[1024,128]{1,0:T(8,128)}) custom-call(f32[1024,128]{1,0:T(8,128)S(1)} %get-tuple-element.13.att_ref, f32[1024,128]{1,0:T(8,128)S(1)} %get-tuple-element.14.gv_ref, f32[2,4,256,128]{3,2,1,0:T(8,128)S(1)} %get-tuple-element.15.push_ref, ...), custom_call_target="tpu_custom_call" | custom-call | tf_op jit(solution)/shard_map/pallas_call | solution.py:463

commit v5 on v4

--- a/solution.py
+++ b/solution.py
@@ -63,9 +63,8 @@
     q_hbm, k_hbm, v_hbm, c_hbm, q_gain_hbm, k_gain_hbm,
     att_ref, gv_ref, push_ref, base_ref, mean_ref,
     raw, gains, unit, other, turned, split, first, second, mix, score, weight, scales,
-    z_send, z_recv, part_send, part_recv, line_scale, staged_unit, peer_unit, peer_other,
-    peer_split,
-    states, peer, chip_sum, gathered, prefixes, entering, passed, received,
+    z_send, z_recv, z_cross, part_send, part_recv, line_scale, bare, peer_bare, peer_other,
+    peer_split, peer_turned, states, chip_sum, gathered, prefixes, entering, passed, received,
     load_sem, z_sems, part_sems, push_sems, core_sems, scan_sems,
 ):
     chips = n_seq // 2
@@ -132,6 +131,16 @@
         for to in heads_on:
             share_copy(slot, to).start()
 
+    def cross_copy(to):
+        return pltpu.make_async_remote_copy(
+            src_ref=z_send.at[0],
+            dst_ref=z_cross.at[head],
+            send_sem=z_sems.at[4],
+            recv_sem=z_sems.at[5],
+            device_id=(peer_seq, to),
+            device_id_type=MESH,
+        )
+
     def part_copy(kind, device):
         return pltpu.make_async_remote_copy(
             src_ref=part_send.at[kind],
@@ -158,7 +167,10 @@
     share_sums(0, query_squares, key_squares)
 
     pl.semaphore_wait(barrier, len(greeted))
-    send_shares(0)
+    for to in heads_on:
+        share_copy(0, to).start()
+        cross_copy(to).start()
+    cross_copy(head).start()
 
     loads[2].wait()
     loads[3].wait()
@@ -171,7 +183,7 @@
         other[1, h] = raw[2, rows_of(h), :]
     for i in range(2):
         for h in range(heads):
-            unit[i, h] = raw[i, rows_of(h), :] * gains[i, pl.ds(h, 1), :]
+            bare[i, h] = raw[i, rows_of(h), :] * gains[i, pl.ds(h, 1), :]
 
     pushes = [
         pltpu.make_async_remote_copy(
@@ -183,11 +195,9 @@
             device_id_type=MESH,
         )
         for i, (src, dst) in enumerate(
-            ((other.at[1 - core], peer_other), (staged_unit, peer_unit))
+            ((other, peer_other), (bare, peer_bare))
         )
     ]
-    for h in range(heads):
-        staged_unit[h] = unit[1 - core, h]
     for push in pushes:
         push.start()
 
@@ -209,39 +219,51 @@
 
     lax.fori_loop(0, heads, mixing, 0)
 
-    total = await_shares(0)
-    scale = lax.rsqrt(total / width + EPSILON)
-    line_scale[...] = scale
-    for i in range(2):
-        scales[i] = down_rows(scale, i, tokens)
+    for push in pushes:
+        push.wait_recv()
+
+    def turning_peer(h, _):
+        peer_turned[h] = left_parts(peer_other[1 - core, h].T, 1)
+        return 0
+
+    lax.fori_loop(0, heads, turning_peer, 0)
+
+    def scale_of(total):
+        return lax.rsqrt(total / width + EPSILON)
 
     def at_head(h):
         return pl.ds(h * depth, depth)
 
-    def block_state(which, h):
-        normed = unit[1 - which, h] * scales[1 - which]
-        unit[1 - which, h] = normed
-        states[which, at_head(h), :] = dot(turned[1 - which, h], right_parts(normed, 0), NN)
-
-    def to_partner(src, dst, phase, h):
+    pairs = tokens // 128
+
+    def of_kind(lines, first_kind):
+        return jnp.where(first_kind, lines[:pairs, :], lines[pairs:, :])
+
+    scale = scale_of(await_shares(0))
+    pltpu.make_async_copy(z_cross, z_cross, z_sems.at[5]).wait()
+    peer_scale = scale_of(jnp.sum(z_cross[...], axis=0))
+    line_scale[...] = scale
+    down = down_rows(of_kind(scale, core == 1), 0, tokens)
+    peer_down = down_rows(of_kind(peer_scale, core == 1), 0, tokens)
+    scales[1 - core] = down
+    for h in range(heads):
+        normed = right_parts(bare[1 - core, h] * down, 0)
+        peer_normed = right_parts(peer_bare[1 - core, h] * peer_down, 0)
+        chip_sum[at_head(h), :] = dot(
+            jnp.concatenate([turned[1 - core, h], peer_turned[h]], axis=1),
+            jnp.concatenate([normed, peer_normed], axis=0),
+            NN,
+        )
+
+    def to_partner(src, dst, h):
         return pltpu.make_async_remote_copy(
             src_ref=src.at[at_head(h)],
             dst_ref=dst.at[at_head(h)],
-            send_sem=core_sems.at[phase, 0, h],
-            recv_sem=core_sems.at[phase, 1, h],
+            send_sem=core_sems.at[0, h],
+            recv_sem=core_sems.at[1, h],
             device_id=partner,
             device_id_type=MESH,
         )
-
-    swaps = [to_partner(states.at[1 - core], peer, 0, h) for h in range(heads)]
-    for h in range(heads):
-        block_state(1 - core, h)
-        swaps[h].start()
-    for h in range(heads):
-        block_state(core, h)
-    for h in range(heads):
-        swaps[h].wait_recv()
-        chip_sum[at_head(h), :] = states[core, at_head(h), :] + peer[at_head(h), :]
 
     def scan_rows(c):
         return pl.ds(pl.multiple_of(c * share, share), share)
@@ -265,12 +287,16 @@
     gathered[chip] = chip_sum[scan_rows(chip), :]
 
     def scoring(h, _):
+        for i in range(2):
+            unit[i, h] = bare[i, h] * scales[i]
+        states[pl.ds(pl.multiple_of(h * depth, depth), depth), :] = dot(
+            turned[1 - core, h], right_parts(unit[1 - core, h], 0), NN
+        )
         score[h] = jnp.where(causal, product(unit[0, h], unit[1, h], NT), 0.0)
-        peer_split[h] = left_parts(peer_other[h], 1)
+        peer_split[h] = left_parts(peer_other[core, h], 1)
         return 0
 
-    for push in pushes:
-        push.wait_recv()
+    scales[core] = down_rows(of_kind(scale, core == 0), 0, tokens)
     lax.fori_loop(0, heads, scoring, 0)
     await_scan(0)
 
@@ -300,9 +326,9 @@
     send_shares(1)
     await_scan(1)
 
-    hands = [to_partner(passed, received, 1, h) for h in range(heads)]
-    for h in range(heads):
-        passed[at_head(h), :] = entering[at_head(h), :] + states[core, at_head(h), :]
+    hands = [to_partner(passed, received, h) for h in range(heads)]
+    for h in range(heads):
+        passed[at_head(h), :] = entering[at_head(h), :] + states[at_head(h), :]
         hands[h].start()
 
     def apply_first(which, state):
@@ -319,7 +345,7 @@
         pushed = dot(split[core, h], right_parts(entering[at_head(h), :], 0), NN)
         second[core, h] += pushed
         own_inner += unit[core, h] * pushed
-        peer_inner += peer_unit[h] * dot(peer_split[h], right_parts(passed[at_head(h), :], 0), NN)
+        peer_inner += peer_bare[core, h] * dot(peer_split[h], right_parts(passed[at_head(h), :], 0), NN)
     for kind, of_one in enumerate((own_inner, peer_inner)):
         sums = lane_sums(of_one)
         for j in range(tokens // 128):
@@ -350,19 +376,18 @@
     pltpu.make_async_copy(part_recv.at[1], part_recv.at[1], part_sems.at[3]).wait()
     own_part = jnp.sum(part_recv[0], axis=0)
     peer_part = jnp.sum(part_recv[1], axis=0)
-    pairs = tokens // 128
     for i in range(2):
         rows = slice(pairs * i, pairs * (i + 1))
         part = jnp.where(core == i, own_part, peer_part * line_scale[rows, :])
         mean_ref[rows, :] = (inside_total[rows, :] + part) / width
 
     for h in range(heads):
-        swaps[h].wait_send()
         hands[h].wait_send()
     for push in pushes:
         push.wait_send()
     pltpu.make_async_copy(others_here, others_here, part_sems.at[0]).wait()
     pltpu.make_async_copy(part_recv.at[1], part_recv.at[1], part_sems.at[2]).wait()
+    pltpu.make_async_copy(z_cross, z_cross, z_sems.at[4]).wait()
     for slot in range(2):
         all_of = z_recv.at[slot, pl.ds(0, n_head - 1)]
         pltpu.make_async_copy(all_of, all_of, z_sems.at[2 * slot]).wait()
@@ -430,14 +455,15 @@
             pltpu.VMEM((2, tokens, depth), F32),
             pltpu.VMEM((2, 2 * tokens // 128, 128), F32),
             pltpu.VMEM((2, n_head, 2 * tokens // 128, 128), F32),
+            pltpu.VMEM((n_head, 2 * tokens // 128, 128), F32),
             pltpu.VMEM((2, tokens // 128, 128), F32),
             pltpu.VMEM((2, n_head, tokens // 128, 128), F32),
             pltpu.VMEM((2 * tokens // 128, 128), F32),
-            pltpu.VMEM(both[1:], F32),
-            pltpu.VMEM(both[1:], F32),
-            pltpu.VMEM(both[1:], F32),
+            pltpu.VMEM(both, F32),
+            pltpu.VMEM(both, F32),
+            pltpu.VMEM(both, F32),
             pltpu.VMEM((heads, tokens, 3 * depth), BF16),
-            pltpu.VMEM((2, *states), F32),
+            pltpu.VMEM((heads, depth, 3 * tokens), BF16),
             pltpu.VMEM(states, F32),
             pltpu.VMEM(states, F32),
             pltpu.VMEM(per_owner, F32),
@@ -446,10 +472,10 @@
             pltpu.VMEM(states, F32),
             pltpu.VMEM(states, F32),
             pltpu.SemaphoreType.DMA((6,)),
+            pltpu.SemaphoreType.DMA((6,)),
             pltpu.SemaphoreType.DMA((4,)),
             pltpu.SemaphoreType.DMA((4,)),
-            pltpu.SemaphoreType.DMA((4,)),
-            pltpu.SemaphoreType.DMA((2, 2, heads)),
+            pltpu.SemaphoreType.DMA((2, heads)),
             pltpu.SemaphoreType.DMA((4,)),
         ],
         compiler_params=pltpu.CompilerParams(

time: 55.3 us -> 53.5 us (0.967)
  Pallas kernels: 54.5 us -> 52.7 us
    pallas_call x1, Pallas kernels: 53.2 us -> 51.4 us  [local(): pl.pallas_call(functools.partial(kernel, n_seq, n_head, heads, tokens, de...]
where the time goes in v5:
time: 53.5 us; the launch traced here: 53.4 us
  Pallas kernels  52.7 us (99%)
  between operations  0.64 us (1%)
    pallas_call x1, Pallas kernels, local(): pl.pallas_call(functools.partial(kernel, n_seq, n_head, heads, tokens, de...  51.4 us
    pallas_call x1, Pallas kernels, local(): pl.pallas_call(functools.partial(leave, heads, tokens), out_shape=[jax.Sh...  1.35 us

profile of v5, /device:TPU:1, one launch (start us, length us, event | category | flops | bytes accessed | tf_op | source)
XLA Modules:
  0.0 53.4 jit_solution(18094318234461456644)
XLA Ops:
  0.6 51.4 %shard_map.93 = (f32[1024,128]{1,0:T(8,128)S(1)}, f32[1024,128]{1,0:T(8,128)S(1)}, f32[2,4,256,128]{3,2,1,0:T(8,128)S(1)}, f32[2,4,256,128]{3,2,1,0:T(8,128)S(1)}, f32[4,128]{1,0:T(4,128)S(1)}) custom-call(f32[1024,128]{1,0:T(8,128)} %bitcast.8, f32[1024,128]{1,0:T(8,128)} %bitcast.9, f32[1024,128]{1,0:T(8,128)} %bitcast.10, f32[1024,128]{1,0:T(8,128)} %bitcast.11, ...), custom_call_target="tpu_custom_call" | custom-call | tf_op jit(solution)/shard_map/pallas_call | solution.py:435
  52.0 1.3 %shard_map.94 = (f32[1024,128]{1,0:T(8,128)}, f32[1024,128]{1,0:T(8,128)}, f32[1024,128]{1,0:T(8,128)}, f32[1024,128]{1,0:T(8,128)}) custom-call(f32[1024,128]{1,0:T(8,128)S(1)} %get-tuple-element.13.att_ref, f32[1024,128]{1,0:T(8,128)S(1)} %get-tuple-element.14.gv_ref, f32[2,4,256,128]{3,2,1,0:T(8,128)S(1)} %get-tuple-element.15.push_ref, ...), custom_call_target="tpu_custom_call" | custom-call | tf_op jit(solution)/shard_map/pallas_call | solution.py:489

commit v6 on v5

--- a/solution.py
+++ b/solution.py
@@ -65,7 +65,7 @@
     raw, gains, unit, other, turned, split, first, second, mix, score, weight, scales,
     z_send, z_recv, z_cross, part_send, part_recv, line_scale, bare, peer_bare, peer_other,
     peer_split, peer_turned, states, chip_sum, gathered, prefixes, entering, passed, received,
-    load_sem, z_sems, part_sems, push_sems, core_sems, scan_sems,
+    load_sem, z_sems, part_sems, push_sems, core_sems, scan_sems, give_sems,
 ):
     chips = n_seq // 2
     share = heads * depth // chips
@@ -80,9 +80,6 @@
         pltpu.make_async_copy(src, gains.at[i], load_sem.at[4 + i])
         for i, src in enumerate((q_gain_hbm, k_gain_hbm))
     ]
-    for load in loads:
-        load.start()
-
     barrier = pltpu.get_barrier_semaphore()
 
     chips_x = min(CHIPS_X, chips)
@@ -95,16 +92,20 @@
     others = [
         lax.rem(chip_y + dy, chips_y) * chips_x + lax.rem(chip_x + dx, chips_x) for dy, dx in steps
     ]
-    heads_on = [
-        lax.rem(head + d, n_head)
-        for d in sorted(range(1, n_head), key=lambda d: -min(d, n_head - d))
-    ]
+    turns = sorted(range(1, n_head), key=lambda d: -min(d, n_head - d))
+    heads_on = [lax.rem(head + d, n_head) for d in turns]
     peer_seq = 2 * chip + 1 - core
     partner = (peer_seq, head)
-    greeted = [(seq, to) for to in heads_on] + [(2 * to + core, head) for to in others]
-    greeted += [(peer_seq, to) for to in heads_on] + [partner]
-    for device in greeted:
+    greeted = [(0, partner)]
+    for d, to in zip(turns, heads_on):
+        greeted += [(min(d, n_head - d), (at, to)) for at in (seq, peer_seq)]
+    for (dy, dx), to in zip(steps, others):
+        hops = min(dy, chips_y - dy) + min(dx, chips_x - dx)
+        greeted.append((hops, (2 * to + core, head)))
+    for _, device in sorted(greeted, key=lambda pair: -pair[0]):
         pl.semaphore_signal(barrier, inc=1, device_id=device, device_id_type=MESH)
+    for load in loads:
+        load.start()
 
     def rows_of(h):
         return pl.ds(h, tokens, stride=heads)
@@ -268,22 +269,23 @@
     def scan_rows(c):
         return pl.ds(pl.multiple_of(c * share, share), share)
 
-    def scan_copy(src, dst, phase, to):
+    def scan_copy(src, dst, send_sem, recv_sem, to):
         return pltpu.make_async_remote_copy(
             src_ref=src,
             dst_ref=dst,
-            send_sem=scan_sems.at[2 * phase],
-            recv_sem=scan_sems.at[2 * phase + 1],
+            send_sem=send_sem,
+            recv_sem=recv_sem,
             device_id=(2 * to + core, head),
             device_id_type=MESH,
         )
 
-    def await_scan(phase):
-        all_of = gathered.at[pl.ds(0, chips - 1)]
-        pltpu.make_async_copy(all_of, all_of, scan_sems.at[2 * phase + 1]).wait()
+    per_head = chips // heads
+    block = chip // per_head
 
     for to in others:
-        scan_copy(chip_sum.at[scan_rows(to)], gathered.at[chip], 0, to).start()
+        scan_copy(
+            chip_sum.at[scan_rows(to)], gathered.at[chip], scan_sems.at[0], scan_sems.at[1], to
+        ).start()
     gathered[chip] = chip_sum[scan_rows(chip), :]
 
     def scoring(h, _):
@@ -298,7 +300,8 @@
 
     scales[core] = down_rows(of_kind(scale, core == 0), 0, tokens)
     lax.fori_loop(0, heads, scoring, 0)
-    await_scan(0)
+    all_others = gathered.at[pl.ds(0, chips - 1)]
+    pltpu.make_async_copy(all_others, all_others, scan_sems.at[1]).wait()
 
     running = jnp.zeros((share, depth), F32)
     for i in range(chips):
@@ -307,8 +310,16 @@
         running = running + gathered[c]
 
     for to in others:
-        scan_copy(prefixes.at[to], entering.at[scan_rows(chip)], 1, to).start()
-    entering[scan_rows(chip), :] = prefixes[chip]
+        scan_copy(
+            prefixes.at[to],
+            entering.at[scan_rows(chip)],
+            give_sems.at[heads],
+            give_sems.at[block],
+            to,
+        ).start()
+    pltpu.make_async_copy(
+        prefixes.at[chip], entering.at[scan_rows(chip)], give_sems.at[block]
+    ).start()
 
     def inside(h, _):
         first[0, h] = product(score[h], other[1, h], NN)
@@ -324,13 +335,6 @@
             inner[i] += unit[i, h] * second[i, h]
     share_sums(1, *inner)
     send_shares(1)
-    await_scan(1)
-
-    hands = [to_partner(passed, received, h) for h in range(heads)]
-    for h in range(heads):
-        passed[at_head(h), :] = entering[at_head(h), :] + states[at_head(h), :]
-        hands[h].start()
-
     def apply_first(which, state):
         def body(h, _):
             held = state[pl.ds(pl.multiple_of(h * depth, depth), depth), :]
@@ -341,11 +345,19 @@
 
     own_inner = jnp.zeros((tokens, depth), F32)
     peer_inner = jnp.zeros((tokens, depth), F32)
-    for h in range(heads):
-        pushed = dot(split[core, h], right_parts(entering[at_head(h), :], 0), NN)
+    for far in sorted(range(heads), key=lambda k: -min(k, heads - k)):
+        h = lax.rem(block + far, heads)
+        here = pl.ds(pl.multiple_of(h * depth, depth), depth)
+        one_head = gathered.at[pl.ds(0, per_head)]
+        pltpu.make_async_copy(one_head, one_head, give_sems.at[h]).wait()
+        held = entering[here, :]
+        next_held = held + states[here, :]
+        passed[here, :] = next_held
+        pushed = dot(split[core, h], right_parts(held, 0), NN)
         second[core, h] += pushed
         own_inner += unit[core, h] * pushed
-        peer_inner += peer_bare[core, h] * dot(peer_split[h], right_parts(passed[at_head(h), :], 0), NN)
+        peer_inner += peer_bare[core, h] * dot(peer_split[h], right_parts(next_held, 0), NN)
+    hands = [to_partner(passed, received, h) for h in range(heads)]
     for kind, of_one in enumerate((own_inner, peer_inner)):
         sums = lane_sums(of_one)
         for j in range(tokens // 128):
@@ -355,6 +367,8 @@
         part_copy(1, (peer_seq, to)).start()
     part_copy(1, partner).start()
     part_recv[0, head] = part_send[0]
+    for hand in hands:
+        hand.start()
 
     for h in range(heads):
         hands[h].wait_recv()
@@ -391,9 +405,8 @@
     for slot in range(2):
         all_of = z_recv.at[slot, pl.ds(0, n_head - 1)]
         pltpu.make_async_copy(all_of, all_of, z_sems.at[2 * slot]).wait()
-    for phase in range(2):
-        all_of = gathered.at[pl.ds(0, chips - 1)]
-        pltpu.make_async_copy(all_of, all_of, scan_sems.at[2 * phase]).wait()
+    for sem in (scan_sems.at[0], give_sems.at[heads]):
+        pltpu.make_async_copy(all_others, all_others, sem).wait()
 
 
 def leave(
@@ -476,7 +489,8 @@
             pltpu.SemaphoreType.DMA((4,)),
             pltpu.SemaphoreType.DMA((4,)),
             pltpu.SemaphoreType.DMA((2, heads)),
-            pltpu.SemaphoreType.DMA((4,)),
+            pltpu.SemaphoreType.DMA((2,)),
+            pltpu.SemaphoreType.DMA((heads + 1,)),
         ],
         compiler_params=pltpu.CompilerParams(
             collective_id=0, has_side_effects=True, vmem_limit_bytes=48 * 1024 * 1024

time: 53.5 us -> 53.4 us (level)
  no operation moved by 1% of the time
where the time goes in v6:
time: 53.4 us; the launch traced here: 53.2 us
  Pallas kernels  52.6 us (99%)
  between operations  0.64 us (1%)
    pallas_call x1, Pallas kernels, local(): pl.pallas_call(functools.partial(kernel, n_seq, n_head, heads, tokens, de...  51.3 us
    pallas_call x1, Pallas kernels, local(): pl.pallas_call(functools.partial(leave, heads, tokens), out_shape=[jax.Sh...  1.35 us

profile of v6, /device:TPU:1, one launch (start us, length us, event | category | flops | bytes accessed | tf_op | source)
XLA Modules:
  0.0 53.2 jit_solution(13385237524156065529)
XLA Ops:
  0.6 51.3 %shard_map.93 = (f32[1024,128]{1,0:T(8,128)S(1)}, f32[1024,128]{1,0:T(8,128)S(1)}, f32[2,4,256,128]{3,2,1,0:T(8,128)S(1)}, f32[2,4,256,128]{3,2,1,0:T(8,128)S(1)}, f32[4,128]{1,0:T(4,128)S(1)}) custom-call(f32[1024,128]{1,0:T(8,128)} %bitcast.8, f32[1024,128]{1,0:T(8,128)} %bitcast.9, f32[1024,128]{1,0:T(8,128)} %bitcast.10, f32[1024,128]{1,0:T(8,128)} %bitcast.11, ...), custom_call_target="tpu_custom_call" | custom-call | tf_op jit(solution)/shard_map/pallas_call | solution.py:448
  51.9 1.3 %shard_map.94 = (f32[1024,128]{1,0:T(8,128)}, f32[1024,128]{1,0:T(8,128)}, f32[1024,128]{1,0:T(8,128)}, f32[1024,128]{1,0:T(8,128)}) custom-call(f32[1024,128]{1,0:T(8,128)S(1)} %get-tuple-element.13.att_ref, f32[1024,128]{1,0:T(8,128)S(1)} %get-tuple-element.14.gv_ref, f32[2,4,256,128]{3,2,1,0:T(8,128)S(1)} %get-tuple-element.15.push_ref, ...), custom_call_target="tpu_custom_call" | custom-call | tf_op jit(solution)/shard_map/pallas_call | solution.py:503

commit v7 on v6

--- a/solution.py
+++ b/solution.py
@@ -247,14 +247,37 @@
     down = down_rows(of_kind(scale, core == 1), 0, tokens)
     peer_down = down_rows(of_kind(peer_scale, core == 1), 0, tokens)
     scales[1 - core] = down
-    for h in range(heads):
+    def scan_rows(c):
+        return pl.ds(pl.multiple_of(c * share, share), share)
+
+    def scan_copy(src, dst, send_sem, recv_sem, to):
+        return pltpu.make_async_remote_copy(
+            src_ref=src,
+            dst_ref=dst,
+            send_sem=send_sem,
+            recv_sem=recv_sem,
+            device_id=(2 * to + core, head),
+            device_id_type=MESH,
+        )
+
+    per_head = chips // heads
+    block = chip // per_head
+
+    for far in sorted(range(heads), key=lambda k: -min(k, heads - k)):
+        h = lax.rem(block + far, heads)
         normed = right_parts(bare[1 - core, h] * down, 0)
         peer_normed = right_parts(peer_bare[1 - core, h] * peer_down, 0)
-        chip_sum[at_head(h), :] = dot(
+        chip_sum[pl.ds(pl.multiple_of(h * depth, depth), depth), :] = dot(
             jnp.concatenate([turned[1 - core, h], peer_turned[h]], axis=1),
             jnp.concatenate([normed, peer_normed], axis=0),
             NN,
         )
+        spots = range(per_head) if far else range(1, per_head)
+        for j in sorted(spots, key=lambda j: -min(j % CHIPS_X, CHIPS_X - j % CHIPS_X)):
+            to = h * per_head + lax.rem(chip + j, per_head)
+            scan_copy(
+                chip_sum.at[scan_rows(to)], gathered.at[chip], scan_sems.at[0], scan_sems.at[1], to
+            ).start()
 
     def to_partner(src, dst, h):
         return pltpu.make_async_remote_copy(
@@ -266,26 +289,6 @@
             device_id_type=MESH,
         )
 
-    def scan_rows(c):
-        return pl.ds(pl.multiple_of(c * share, share), share)
-
-    def scan_copy(src, dst, send_sem, recv_sem, to):
-        return pltpu.make_async_remote_copy(
-            src_ref=src,
-            dst_ref=dst,
-            send_sem=send_sem,
-            recv_sem=recv_sem,
-            device_id=(2 * to + core, head),
-            device_id_type=MESH,
-        )
-
-    per_head = chips // heads
-    block = chip // per_head
-
-    for to in others:
-        scan_copy(
-            chip_sum.at[scan_rows(to)], gathered.at[chip], scan_sems.at[0], scan_sems.at[1], to
-        ).start()
     gathered[chip] = chip_sum[scan_rows(chip), :]
 
     def scoring(h, _):

time: 53.4 us -> 52.9 us (level)
  no operation moved by 1% of the time
where the time goes in v7:
time: 52.9 us; the launch traced here: 52.8 us
  Pallas kernels  52.1 us (98%)
  between operations  0.64 us (1%)
    pallas_call x1, Pallas kernels, local(): pl.pallas_call(functools.partial(kernel, n_seq, n_head, heads, tokens, de...  50.8 us
    pallas_call x1, Pallas kernels, local(): pl.pallas_call(functools.partial(leave, heads, tokens), out_shape=[jax.Sh...  1.35 us

profile of v7, /device:TPU:1, one launch (start us, length us, event | category | flops | bytes accessed | tf_op | source)
XLA Modules:
  0.0 52.8 jit_solution(11178617905150346028)
XLA Ops:
  0.6 50.8 %shard_map.93 = (f32[1024,128]{1,0:T(8,128)S(1)}, f32[1024,128]{1,0:T(8,128)S(1)}, f32[2,4,256,128]{3,2,1,0:T(8,128)S(1)}, f32[2,4,256,128]{3,2,1,0:T(8,128)S(1)}, f32[4,128]{1,0:T(4,128)S(1)}) custom-call(f32[1024,128]{1,0:T(8,128)} %bitcast.8, f32[1024,128]{1,0:T(8,128)} %bitcast.9, f32[1024,128]{1,0:T(8,128)} %bitcast.10, f32[1024,128]{1,0:T(8,128)} %bitcast.11, ...), custom_call_target="tpu_custom_call" | custom-call | tf_op jit(solution)/shard_map/pallas_call | solution.py:451
  51.4 1.3 %shard_map.94 = (f32[1024,128]{1,0:T(8,128)}, f32[1024,128]{1,0:T(8,128)}, f32[1024,128]{1,0:T(8,128)}, f32[1024,128]{1,0:T(8,128)}) custom-call(f32[1024,128]{1,0:T(8,128)S(1)} %get-tuple-element.13.att_ref, f32[1024,128]{1,0:T(8,128)S(1)} %get-tuple-element.14.gv_ref, f32[2,4,256,128]{3,2,1,0:T(8,128)S(1)} %get-tuple-element.15.push_ref, ...), custom_call_target="tpu_custom_call" | custom-call | tf_op jit(solution)/shard_map/pallas_call | solution.py:506
